TPU v7x, 512 devices: a whole 4x4x16 slice. The times are simulated.
512 devices in a mesh: query: 4 (over x), cand: 32 (over z_hi, y, core), tensor: 4 (over z_lo).
Axes of the slice: x: 4, y: 4, z: 16 (z_hi: 4, z_lo: 4; z = z_hi * 4 + z_lo), core: 2. Of those that a mesh axis runs over, the one named last changes fastest.
Arguments:
- cand_states: bfloat16 [131072, 2048], P(('query', 'cand'), 'tensor'), parts along dimension 0, may hold values from -6 to 6
- prefix_states: bfloat16 [256, 2048], P(('query', 'cand'), 'tensor'), parts along dimension 0, may hold values from -6 to 6
- norm_gain: float32 [2048], replicated, may hold values from 0.5 to 1.5
- w_query: bfloat16 [2048, 1024], P(None, 'tensor'), may hold values from -1 to 1
- w_key: bfloat16 [2048, 256], P(None, 'tensor'), may hold values from -1 to 1
- w_value: bfloat16 [2048, 256], P(None, 'tensor'), may hold values from -0.125 to 0.125
- w_out: bfloat16 [1024, 2048], P('tensor'), may hold values from -1.5 to 1.5
- cand_lengths: int32 [1024], P(('query', 'cand')), parts along dimension 0, may hold values from 32 to 128, as said below
Outputs:
- attn_out: bfloat16 [131072, 2048], P(('query', 'cand', 'tensor')), parts along dimension 0
There are 4 independent parts, one for each index of `query`. A program takes and returns all parts, laid end to end along the dimension named above; an argument that names none is the same for every part. Nothing has to cross between parts.
Inputs may be any that keep to these rules, and one draw needn't show every extreme that they name: `cand_lengths`: some candidate has all 128 slots live.
All inputs are finite; a program needn't handle non-finite values.
Results may differ from a plain program's by a relative error of at most 0.013.
Values may be sent and summed in bfloat16 or wider, within the bound.
A program may use at most 64 MiB of HBM per device.

v0:
```python
import jax
import jax.numpy as jnp
from jax import lax
from jax.sharding import PartitionSpec as P

epsilon = 1e-06
theta_base = 10000.0


def in_one_piece(arrays, axis, dim, along):
    both = jnp.concatenate(arrays, axis=along)
    filled, at, outs = (lax.all_gather(both, axis, axis=dim, tiled=True), 0, [])
    for a in arrays:
        outs.append(lax.slice_in_dim(filled, at, at + a.shape[along], axis=along))
        at += a.shape[along]
    return tuple(outs)


def joined_along(tiles, dim):
    lengths = list(tiles.shape[1:])
    lengths[dim] *= tiles.shape[0]
    return jnp.moveaxis(tiles, 0, dim).reshape(lengths)


def from_everyone(value, axis):
    copies = jnp.broadcast_to(value, (lax.axis_size(axis), *value.shape))
    return lax.all_to_all(copies, axis, split_axis=0, concat_axis=0, tiled=True)


def collect(value, axis, dim):
    return joined_along(from_everyone(value, axis), dim)


def in_one_piece_2(arrays, axis, dim, along):
    ends, at = ([], 0)
    for a in arrays[:-1]:
        at += a.shape[along]
        ends.append(at)
    both = jnp.concatenate(arrays, axis=along)
    return tuple(jnp.split(collect(both, axis, dim), ends, axis=along))


def rotate(values, positions):
    half_size = values.shape[-1] // 2
    frequency = theta_base ** (-jnp.arange(half_size, dtype=jnp.float32) * 2.0 / values.shape[-1])
    angles = positions.astype(jnp.float32)[:, None] * frequency[None, :]
    cosine = jnp.cos(angles)
    sine_part = jnp.sin(angles)
    lower_half = values[:, :half_size]
    upper_half = values[:, half_size:]
    return jnp.concatenate(
        [
            lower_half * cosine - upper_half * sine_part,
            upper_half * cosine + lower_half * sine_part,
        ],
        axis=-1,
    )


def normalize(states, norm_gain):
    values = states.astype(jnp.float32)
    square = jnp.mean(values * values, axis=-1, keepdims=True)
    return (values * lax.rsqrt(square + epsilon) * norm_gain[None, :]).astype(jnp.bfloat16)


def self_scores_of(queries, cand_keys):
    scores = jnp.einsum("cqd,ckd->cqk", queries, cand_keys, preferred_element_type=jnp.float32)
    slots = jnp.arange(scores.shape[1], dtype=jnp.int32)
    causal = slots[:, None] >= slots[None, :]
    return jnp.where(causal[None], scores, -jnp.inf)


def body(cand_states, prefix_states, norm_gain, w_query, w_key, w_value, w_out, cand_lengths):
    cand_full, prefix_full = in_one_piece((cand_states, prefix_states), "tensor", 1, 0)
    normed_cand = normalize(cand_full, norm_gain)
    normed_prefix = normalize(prefix_full, norm_gain)
    cand_count = cand_lengths.shape[0]
    cand_len = cand_full.shape[0] // cand_count
    prefix_rows = prefix_full.shape[0]
    cand_groups = lax.axis_size("cand")
    tensor_size = lax.axis_size("tensor")
    prefix_len = prefix_rows * cand_groups
    head_size = w_query.shape[1]
    cand_pos = prefix_len + jnp.tile(jnp.arange(cand_len, dtype=jnp.int32), cand_count)
    cand_key = jnp.dot(normed_cand, w_key, preferred_element_type=jnp.float32).astype(jnp.bfloat16)
    cand_value = jnp.dot(normed_cand, w_value, preferred_element_type=jnp.float32).astype(
        jnp.bfloat16
    )
    prefix_key = jnp.dot(normed_prefix, w_key, preferred_element_type=jnp.float32).astype(
        jnp.bfloat16
    )
    prefix_value = jnp.dot(normed_prefix, w_value, preferred_element_type=jnp.float32).astype(
        jnp.bfloat16
    )
    query_rows = rotate(
        jnp.dot(normed_cand, w_query, preferred_element_type=jnp.float32), cand_pos
    ) * head_size ** (-0.5)
    queries = query_rows.astype(jnp.bfloat16).reshape(cand_count, cand_len, head_size)
    cand_key, cand_value, prefix_key, prefix_value = in_one_piece_2(
        (cand_key, cand_value, prefix_key, prefix_value), "tensor", 1, 0
    )
    prefix_pos = lax.axis_index("cand") * prefix_rows + jnp.arange(prefix_rows, dtype=jnp.int32)
    prefix_key = rotate(prefix_key.astype(jnp.float32), prefix_pos).astype(jnp.bfloat16)
    cand_keys = (
        rotate(cand_key.astype(jnp.float32), cand_pos)
        .astype(jnp.bfloat16)
        .reshape(cand_count, cand_len, head_size)
    )
    cand_values = cand_value.reshape(cand_count, cand_len, head_size)
    self_scores = self_scores_of(queries, cand_keys)
    highest = self_scores.max(-1)
    weights = jnp.exp(self_scores - highest[..., None])
    highest, divisor, summed = (
        highest,
        weights.sum(-1),
        jnp.einsum(
            "cqk,ckd->cqd",
            weights.astype(jnp.bfloat16),
            cand_values,
            preferred_element_type=jnp.float32,
        ),
    )
    key_piece, value_piece = in_one_piece((prefix_key, prefix_value), "cand", 0, 1)
    prefix_scores = jnp.einsum(
        "cqd,kd->cqk", queries, key_piece, preferred_element_type=jnp.float32
    )
    new_highest = jnp.maximum(highest, prefix_scores.max(-1))
    rescale = jnp.exp(highest - new_highest)
    weights = jnp.exp(prefix_scores - new_highest[..., None])
    divisor = divisor * rescale + weights.sum(-1)
    summed = summed * rescale[..., None] + jnp.einsum(
        "cqk,kd->cqd", weights.astype(jnp.bfloat16), value_piece, preferred_element_type=jnp.float32
    )
    highest, divisor, summed = (new_highest, divisor, summed)
    slots = jnp.arange(cand_len, dtype=jnp.int32)
    live_rows = slots[None, :] < cand_lengths[:, None]
    head_rows = jnp.where(live_rows[..., None], summed / divisor[..., None], 0.0)
    head_rows = head_rows.reshape(cand_count * cand_len, head_size).astype(jnp.bfloat16)
    row_count = head_rows.shape[0] // tensor_size
    all_heads = lax.all_to_all(head_rows, "tensor", split_axis=0, concat_axis=1, tiled=True)
    full_out = lax.all_gather(w_out, "tensor", axis=0, tiled=True)
    summed_out = jnp.zeros((row_count, full_out.shape[1]), jnp.float32)
    for head_index in range(tensor_size):
        head_term = jnp.dot(
            all_heads[:, head_index * head_size : (head_index + 1) * head_size],
            full_out[head_index * head_size : (head_index + 1) * head_size],
            preferred_element_type=jnp.float32,
        )
        summed_out = summed_out + lax.optimization_barrier(head_term.astype(jnp.bfloat16)).astype(
            jnp.float32
        )
    return summed_out.astype(jnp.bfloat16)


def solution(mesh):
    in_specs = (
        P(("query", "cand"), "tensor"),
        P(("query", "cand"), "tensor"),
        P(),
        P(None, "tensor"),
        P(None, "tensor"),
        P(None, "tensor"),
        P("tensor", None),
        P(("query", "cand")),
    )
    out_specs = P(("query", "cand", "tensor"), None)
    return jax.shard_map(body, mesh=mesh, in_specs=in_specs, out_specs=out_specs, check_vma=False)
```

profile of v0, /device:TPU:1, one launch (start us, length us, event | category | flops | bytes accessed | tf_op | source)
XLA Modules:
  0.0 256.7 jit_solution(11628794614377574297)
XLA Ops:
  6.5 2.4 pad_maximum_fusion
  8.9 95.2 %all-gather.4.cloned.1.call-done = bf16[1026,2048]{1,0:T(8,128)(2,1)} async-done(((bf16[1026,512]{1,0:T(8,128)(2,1)}), bf16[1026,2048]{1,0:T(8,128)(2,1)}) %all-gather.4.cloned.1.call-update) | async-done | bytes 4202512 | tf_op jit(solution)/shard_map/all_gather | solution.py:12
  104.2 3.1 %fusion = f32[1024]{0:T(1024)S(1)} fusion(bf16[1026,2048]{1,0:T(8,128)(2,1)} %all-gather.4.cloned.1.call-done), kind=kLoop, calls=%fused_computation.2 | loop fusion | flops 6290432 | bytes 4198400 | tf_op jit(solution)/shard_map/reduce_sum | solution.py:62
  107.3 2.9 %fusion.2 = bf16[1024,2048]{1,0:T(8,128)(2,1)S(1)} fusion(f32[2048]{0:T(1024)S(1)} %copy-done.5, f32[1024]{0:T(1024)S(1)} %add_rsqrt_fusion, bf16[1026,2048]{1,0:T(8,128)(2,1)} %all-gather.4.cloned.1.call-done), kind=kLoop, calls=%fused_computation.4 | loop fusion | flops 8388608 | bytes 8400896 | tf_op jit(solution)/shard_map/convert_element_type | solution.py:63
  110.2 1.4 convolution_convert_fusion.4
  111.6 1.4 convolution_convert_fusion.5
  113.0 0.9 fusion.42
  113.9 1.0 convolution_convert_fusion.7
  115.0 1.0 convolution_convert_fusion.6
  116.3 1.2 broadcast_in_dim.24
  117.4 3.5 %all-to-all-start = ((bf16[4,2052,64]{1,2,0:T(8,128)(2,1)}), bf16[4,2052,64]{1,2,0:T(8,128)(2,1)S(1)}, u32[]{:S(2)}, u32[]{:S(2)}) async-start(bf16[4,2052,64]{1,2,0:T(8,128)(2,1)} %broadcast_in_dim.24), calls=%async_computation | async-start | bytes 2228224 | tf_op jit(solution)/shard_map/all_to_all | solution.py:27
  121.0 0.7 all-gather.6.cloned.1.call-update
  121.9 4.4 %fusion.68 = f32[1024,256]{1,0:T(8,128)} fusion(bf16[1024,2048]{1,0:T(8,128)(2,1)} %copy-done.1, bf16[2048,256]{1,0:T(8,128)(2,1)S(1)} %copy-done), kind=kOutput, calls=%fused_computation.100 | convolution fusion | flops 1073741824 | bytes 6291456 | tf_op jit(solution)/shard_map/dot_general | solution.py:96
  126.3 21.3 %all-to-all-done = bf16[4,2052,64]{1,2,0:T(8,128)(2,1)S(1)} async-done(((bf16[4,2052,64]{1,2,0:T(8,128)(2,1)}), bf16[4,2052,64]{1,2,0:T(8,128)(2,1)S(1)}, u32[]{:S(2)}, u32[]{:S(2)}) %all-to-all-start) | async-done | bytes 1050656 | tf_op jit(solution)/shard_map/all_to_all | solution.py:27
  147.6 1.0 fusion.62
  148.7 0.9 fusion.64
  149.8 1.2 copy.45
  151.6 65.6 %all-gather = bf16[32,2,512]{2,1,0:T(2,128)(2,1)S(1)} all-gather(bf16[1,2,512]{2,1,0:T(2,128)(2,1)S(1)} %maximum_bitcast_fusion), channel_id=1, replica_groups=mesh['query'=4,'cand'=32,'tensor'=4] {'cand'}, dimensions={0}, use_global_device_ids=true | all-gather | bytes 67584 | tf_op jit(solution)/shard_map/all_gather | solution.py:12
  217.2 1.1 copy.48
  218.4 3.8 %fusion.22 = (bf16[1024,128]{1,0:T(8,128)(2,1)S(1)}, bf16[1024,128]{1,0:T(8,128)(2,1)S(1)}, f32[1024,128]{1,0:T(8,128)S(1)}, f32[1024,128]{1,0:T(8,128)S(1)}) fusion(f32[1024,128]{1,0:T(8,128)S(1)} %copy.45, f32[1024,128]{1,0:T(8,128)S(1)} %copy.44, f32[128]{0:T(128)S(1)} %multiply_power_fusion, f32[1024]{0:T(1024)S(1)} %convert_bitcast_fusion, ...), kind=kLoop, calls=%fused_computation.40 | loop fusion | flops 1966080 | bytes 3674624 | tf_op jit(solution)/shard_map/convert.7
  222.2 0.3 fusion.67
  222.5 0.3 fusion.66
  223.0 0.4 convolution_multiply_fusion
  223.4 0.4 fusion.5
  223.8 1.0 copy.42
  224.8 4.7 %all-to-all-start.1 = ((bf16[4,256,256]{1,2,0:T(8,128)(2,1)}), bf16[4,256,256]{1,2,0:T(8,128)(2,1)S(1)}, u32[]{:S(2)}, u32[]{:S(2)}) async-start(bf16[4,256,256]{1,2,0:T(8,128)(2,1)} %copy.42), calls=%async_computation.1 | async-start | bytes 1048576 | tf_op jit(solution)/shard_map/all_to_all | solution.py:140
  229.5 14.1 %all-to-all-done.1 = bf16[4,256,256]{1,2,0:T(8,128)(2,1)S(1)} async-done(((bf16[4,256,256]{1,2,0:T(8,128)(2,1)}), bf16[4,256,256]{1,2,0:T(8,128)(2,1)S(1)}, u32[]{:S(2)}, u32[]{:S(2)}) %all-to-all-start.1) | async-done | bytes 524320 | tf_op jit(solution)/shard_map/all_to_all | solution.py:140
  243.7 1.8 convolution_convert_fusion.3
  245.5 1.7 convolution_convert_fusion.2
  247.2 0.5 convolution_convert_fusion.1
  247.7 0.5 convolution_convert_fusion
  248.1 1.7 add_convert_fusion
  (43 shorter events, 1.6 us)
Async XLA Ops:
  6.5 115.3 %copy-start = (bf16[2048,256]{1,0:T(8,128)(2,1)S(1)}, bf16[2048,256]{1,0:T(8,128)(2,1)}, u32[]{:S(2)}) copy-start(bf16[2048,256]{1,0:T(8,128)(2,1)} %param.11) | copy-start | bytes 3145732
  6.5 100.7 %copy-start.5 = (f32[2048]{0:T(1024)S(1)}, f32[2048]{0:T(1024)}, u32[]{:S(2)}) copy-start(f32[2048]{0:T(1024)} %param.10) | copy-start | bytes 24580
  6.5 97.6 %all-gather.4.cloned.1.call-start = ((), (), s32[]{:S(2)}) async-start(), calls=%async_computation.2 | async-start | bytes 5283840 | tf_op jit(solution)/shard_map/all_gather | solution.py:12
  107.3 2.9 %copy-start.4 = (bf16[2048,64]{0,1:T(8,128)(2,1)S(1)}, bf16[2048,64]{0,1:T(8,128)(2,1)}, u32[]{:S(2)}) copy-start(bf16[2048,64]{0,1:T(8,128)(2,1)} %param.13) | copy-start | bytes 786436
  110.2 2.8 %copy-start.1 = (bf16[1024,2048]{1,0:T(8,128)(2,1)}, bf16[1024,2048]{1,0:T(8,128)(2,1)S(1)}, u32[]{:S(2)}) copy-start(bf16[1024,2048]{1,0:T(8,128)(2,1)S(1)} %fusion.2) | copy-start | bytes 12582916
  110.2 1.4 copy-start.3
  113.0 8.8 %copy-start.6 = (s32[8]{0:T(128)S(1)}, s32[8]{0:T(128)}, u32[]{:S(2)}) copy-start(s32[8]{0:T(128)} %param.15) | copy-start | bytes 100
  117.4 30.2 %all-to-all-start = ((bf16[4,2052,64]{1,2,0:T(8,128)(2,1)}), bf16[4,2052,64]{1,2,0:T(8,128)(2,1)S(1)}, u32[]{:S(2)}, u32[]{:S(2)}) async-start(bf16[4,2052,64]{1,2,0:T(8,128)(2,1)} %broadcast_in_dim.24), calls=%async_computation | async-start | bytes 2228224 | tf_op jit(solution)/shard_map/all_to_all | solution.py:27
  121.0 108.6 %all-gather.6.cloned.1.call-start = ((), (), s32[]{:S(2)}) async-start(), calls=%async_computation.3 | async-start | bytes 5242880 | tf_op jit(solution)/shard_map/all_gather | solution.py:141
  224.8 18.9 %all-to-all-start.1 = ((bf16[4,256,256]{1,2,0:T(8,128)(2,1)}), bf16[4,256,256]{1,2,0:T(8,128)(2,1)S(1)}, u32[]{:S(2)}, u32[]{:S(2)}) async-start(bf16[4,256,256]{1,2,0:T(8,128)(2,1)} %copy.42), calls=%async_computation.1 | async-start | bytes 1048576 | tf_op jit(solution)/shard_map/all_to_all | solution.py:140
  243.7 3.5 %copy-start.2 = (bf16[1024,2048]{1,0:T(8,128)(2,1)S(1)}, bf16[1024,2048]{1,0:T(8,128)(2,1)}, u32[]{:S(2)}) copy-start(bf16[1024,2048]{1,0:T(8,128)(2,1)} %all-gather.6.cloned.1.call-done) | copy-start | bytes 12582916
Sparse Core Ops, SparseCore 0:
  9.4 94.6 all-gather.3
  123.9 93.5 all-gather.5
where the time goes:
time: 257 us
  waiting for transfers between devices  131 us (51%)
  blocking collectives  65.6 us (26%)
  other arithmetic  15.3 us (6%)
  matrix products  15 us (6%)
  between operations  13.7 us (5%)
  starting transfers between devices  8.3 us (3%)
  local copies, waits for them, and re-layouts  7.31 us (3%)
    all_gather x1, waiting for transfers between devices, in_one_piece(): filled, at, outs = (lax.all_gather(both, axis, axis=dim, tiled=True), 0, [])  95.2 us
    all_gather x1, blocking collectives, in_one_piece(): filled, at, outs = (lax.all_gather(both, axis, axis=dim, tiled=True), 0, [])  65.6 us
    all_to_all x1, waiting for transfers between devices, from_everyone(): return lax.all_to_all(copies, axis, split_axis=0, concat_axis=0, tiled=True)  21.3 us
    all_to_all x1, waiting for transfers between devices, body(): lax.all_to_all(head_rows, 'tensor', split_axis=0, concat_axis=1, tiled=True)  14.1 us
  transfers between devices with their start and end apart: 4, of which 3 were waited for; matrix products, arithmetic and copies ran while one was open for 6% of the time, Pallas kernels for 0%

commit v1 on v0

v1 whole, which is shorter than its diff:
```python
import numpy as np

import jax
import jax.numpy as jnp
from jax import lax
from jax.experimental import pallas as pl
from jax.experimental.pallas import tpu as pltpu
from jax.sharding import PartitionSpec as P

MESH = pl.DeviceIdType.MESH
BF16 = jnp.bfloat16
F32 = jnp.float32
EPS = 1e-06
THETA = 10000.0

NX = 4
NY = 4
NZ = 16
ZL = 4
CL = 128
HS = 256
D = 2048
FC = 512
PRE = 64


def rope_tables():
    half = HS // 2
    freq = (THETA ** (-np.arange(half, dtype=np.float32) * 2.0 / HS)).astype(np.float32)
    cand = (PRE + np.arange(CL)).astype(np.float32)
    core, y, zh, r = np.meshgrid(
        np.arange(2), np.arange(4), np.arange(4), np.arange(2), indexing="ij"
    )
    pre = ((zh * 8 + y * 2 + core) * 2 + r).reshape(-1).astype(np.float32)
    pos = np.concatenate([cand, pre])
    angles = (pos[:, None] * freq[None, :]).astype(np.float32).astype(np.float64)
    return np.cos(angles).astype(np.float32), np.sin(angles).astype(np.float32)


class Links:
    def __init__(self, ssem, rsem):
        self.ssem, self.rsem, self.made = ssem, rsem, []

    def send(self, src, dst, device):
        i = len(self.made)
        copy = pltpu.make_async_remote_copy(
            src_ref=src,
            dst_ref=dst,
            send_sem=self.ssem.at[i],
            recv_sem=self.rsem.at[i],
            device_id=device,
            device_id_type=MESH,
        )
        copy.start()
        self.made.append(copy)
        return copy

    def finish(self):
        for copy in self.made:
            copy.wait_send()


N_SEMS = 120


def kernel(
    states, prefix, gain, wq, wkv, wo, lens, cos_t, sin_t,
    out,
    A, B, xs, xb, pb, pf, xn, kvs, kc, vc, q4, hr, ob, ssem, rsem, lsem,
):
    x = lax.axis_index("query")
    cd = lax.axis_index("cand")
    t = lax.axis_index("tensor")
    zh = cd // 8
    y = (cd // 2) % 4
    c = cd % 2
    z = zh * 4 + t

    def at(xx, yy, zz, cc):
        return (xx, (zz // 4) * 8 + yy * 2 + cc, zz % 4)

    def m4(v):
        return (v + 8) % 4

    def zdev(dz):
        return at(x, y, (z + dz + 32) % 16, c)

    def tdev(k):
        return (x, cd, (t + k) % 4)

    xp, xm = at(m4(x + 1), y, z, c), at(m4(x - 1), y, z, c)
    yp, ym = at(x, m4(y + 1), z, c), at(x, m4(y - 1), z, c)
    yo = at(x, m4(y + 2), z, c)
    mate = at(x, y, z, 1 - c)

    def rows_a(xx, yy, off=0, n=64):
        return pl.ds(pl.multiple_of(64 * (c * 16 + yy * 4 + xx) + off, 32), n)

    def cols_b(xx, yy):
        return pl.ds(pl.multiple_of(128 * (xx * 4 + yy), 128), 128)

    def rows_b(off=0, n=128):
        return pl.ds(pl.multiple_of(128 * c + off, 64), n)

    def slice_a(xx, yy, off=0, n=64):
        return A.at[1:4, rows_a(xx, yy, off, n), :]

    def slice_b(xx, yy, off=0, n=128):
        return B.at[1:4, rows_b(off, n), cols_b(xx, yy)]

    def local(i, src, dst):
        copy = pltpu.make_async_copy(src, dst, lsem.at[i])
        copy.start()
        return copy

    lp = local(0, prefix, pb.at[c, y, z])
    lq = local(1, wq, A.at[0, :, 0:256])
    lkv = local(2, wkv, A.at[0, :, 256:384])
    lo = local(3, wo, B.at[0])
    ls = local(4, states, xs)
    lx = local(5, states.at[pl.ds(pl.multiple_of(256 * t, 256), 256), :], xb.at[t])

    barrier = pltpu.get_barrier_semaphore()
    near = [zdev(d) for d in (-4, -3, -2, -1, 1, 2, 3, 4)]
    near += [xp, xm, yp, ym, yo, mate]
    for device in near:
        pl.semaphore_signal(barrier, inc=1, device_id=device, device_id_type=MESH)
    pl.semaphore_wait(barrier, len(near))

    net = Links(ssem, rsem)

    lp.wait()
    tile = pb.at[c, y, z]
    pz = {d: net.send(tile, tile, zdev(d)) for d in (4, -4, 1, -1, 2, -2, 3, -3)}

    lq.wait()
    lkv.wait()
    pa = []
    for k in (2, 1, 3):
        src = A.at[0, rows_a(x, y), :]
        pa.append(net.send(src, A.at[4 - k, rows_a(x, y), :], tdev(k)))
    lo.wait()
    pbq = []
    for k in (2, 1, 3):
        src = B.at[0, rows_b(), cols_b(x, y)]
        pbq.append(net.send(src, B.at[4 - k, rows_b(), cols_b(x, y)], tdev(k)))

    pz[4].wait_recv()
    pz[-4].wait_recv()
    low = pb.at[c, y, (z + 12) % 16]
    high = pb.at[c, y, (z + 4) % 16]
    pz2 = [net.send(low, low, zdev(d)) for d in (4, 3, 2, 1)]
    pz2 += [net.send(high, high, zdev(d)) for d in (-3, -2, -1)]

    ls.wait()
    st = []
    for cc in range(2):
        part = []
        for k in (2, 1, 3):
            peer = (t + k) % 4
            src = xs.at[pl.ds(pl.multiple_of(256 * peer + 128 * cc, 128), 128), :]
            dst = xb.at[t, pl.ds(128 * cc, 128), :]
            part.append(net.send(src, dst, tdev(k)))
        st.append(part)

    for copy in pa:
        copy.wait_recv()
    own_a, own_b = slice_a(x, y), slice_b(x, y)
    a_xp = net.send(own_a, own_a, xp)
    a_xm = net.send(own_a, own_a, xm)
    for copy in pbq:
        copy.wait_recv()
    b_yp = net.send(own_b, own_b, yp)
    b_ym = net.send(own_b, own_b, ym)
    ya = {0: (net.send(own_a, own_a, yp), net.send(own_a, own_a, ym))}
    xbp = {0: (net.send(own_b, own_b, xp), net.send(own_b, own_b, xm))}

    for d in (-3, -2, -1, 1, 2, 3):
        pz[d].wait_recv()
    for copy in pz2:
        copy.wait_recv()
    line = pb.at[c, y]
    py = [net.send(line, line, d) for d in (yp, ym, yo)]

    def slice_fwd(first, second):
        pass

    a_xp.wait_recv()
    h = slice_a(m4(x - 1), y, 0, 32)
    a_xp2 = net.send(h, h, xp)
    s = slice_a(m4(x - 1), y)
    ya[-1] = (net.send(s, s, yp), net.send(s, s, ym))
    b_yp.wait_recv()
    h = slice_b(x, m4(y - 1), 0, 64)
    b_yp2 = net.send(h, h, yp)
    s = slice_b(x, m4(y - 1))
    xbp[-1] = (net.send(s, s, xp), net.send(s, s, xm))
    a_xm.wait_recv()
    h = slice_a(m4(x + 1), y, 32, 32)
    a_xm2 = net.send(h, h, xm)
    s = slice_a(m4(x + 1), y)
    ya[1] = (net.send(s, s, yp), net.send(s, s, ym))
    b_ym.wait_recv()
    h = slice_b(x, m4(y + 1), 64, 64)
    b_ym2 = net.send(h, h, ym)
    s = slice_b(x, m4(y + 1))
    xbp[1] = (net.send(s, s, xp), net.send(s, s, xm))

    for copy in py:
        copy.wait_recv()
    pm = net.send(pb.at[c], pb.at[c], mate)

    a_xp2.wait_recv()
    a_xm2.wait_recv()
    s = slice_a(m4(x + 2), y)
    ya[2] = (net.send(s, s, yp), net.send(s, s, ym))
    b_yp2.wait_recv()
    b_ym2.wait_recv()
    s = slice_b(x, m4(y + 2))
    xbp[2] = (net.send(s, s, xp), net.send(s, s, xm))

    def set_a(yy):
        return A.at[1:4, pl.ds(pl.multiple_of(64 * (c * 16 + yy * 4), 256), 256), :]

    def set_b(xx):
        return B.at[1:4, rows_b(), pl.ds(pl.multiple_of(512 * xx, 512), 512)]

    mates = [net.send(set_a(y), set_a(y), mate), net.send(set_b(x), set_b(x), mate)]

    fwd = []
    for dx in (0, -1, 1, 2):
        ya[dx][0].wait_recv()
        h = slice_a(m4(x + dx), m4(y - 1), 0, 32)
        fwd.append(net.send(h, h, yp))
        xbp[dx][0].wait_recv()
        h = slice_b(m4(x - 1), m4(y + dx), 0, 64)
        fwd.append(net.send(h, h, xp))
        ya[dx][1].wait_recv()
        h = slice_a(m4(x + dx), m4(y + 1), 32, 32)
        fwd.append(net.send(h, h, ym))
        xbp[dx][1].wait_recv()
        h = slice_b(m4(x + 1), m4(y + dx), 64, 64)
        fwd.append(net.send(h, h, xm))
    for s in (set_a(m4(y - 1)), set_b(m4(x - 1)), set_a(m4(y + 1)), set_b(m4(x + 1))):
        mates.append(net.send(s, s, mate))

    lx.wait()

    def norm_cand(cc):
        rows = pl.ds(128 * cc, 128)
        total = jnp.zeros((128, 1), F32)
        for f in range(4):
            v = xb[f, rows, :].astype(F32)
            total += jnp.sum(v * v, axis=-1, keepdims=True)
        scale = lax.rsqrt(total * (1.0 / D) + EPS)
        for f in range(4):
            v = xb[f, rows, :].astype(F32)
            g = gain[:, FC * f : FC * (f + 1)]
            xn[rows, FC * f : FC * (f + 1)] = (v * scale * g).astype(BF16)

    for copy in st[0]:
        copy.wait_recv()
    norm_cand(0)

    pm.wait_recv()
    for f in range(4):
        for cc in range(2):
            for yy in range(4):
                for hh in range(4):
                    at_row = ((cc * 4 + yy) * 4 + hh) * 8
                    pf[f, at_row : at_row + 8, :] = pb[cc, yy, hh * 4 + f].astype(F32)
    pieces = [
        [pf[f, pl.ds(k, PRE, stride=4), :] for k in range(4)] for f in range(4)
    ]
    total = jnp.zeros((PRE, 1), F32)
    for row in pieces:
        for v in row:
            total += jnp.sum(v * v, axis=-1, keepdims=True)
    scale = lax.rsqrt(total * (1.0 / D) + EPS)
    for f in range(4):
        for k in range(4):
            lo_col = FC * f + 128 * k
            g = gain[:, lo_col : lo_col + 128]
            xn[256:320, lo_col : lo_col + 128] = (pieces[f][k] * scale * g).astype(BF16)

    for copy in fwd:
        copy.wait_recv()
    for s in (set_a(m4(y + 2)), set_b(m4(x + 2))):
        mates.append(net.send(s, s, mate))
    for copy in mates:
        copy.wait_recv()

    def rotate(v, cos, sin):
        a, b = v[:, :128], v[:, 128:]
        return jnp.concatenate([a * cos - b * sin, b * cos + a * sin], axis=-1)

    def project_kv(rows, n, table, key_rows, cc):
        xv = xn[rows, :]
        for pair in range(2):
            w = jnp.concatenate([A[2 * pair, :, 256:384], A[2 * pair + 1, :, 256:384]], axis=-1)
            r = jnp.dot(xv, w, preferred_element_type=F32)
            kvs[2 * pair, 0:n, :] = r[:, :128]
            kvs[2 * pair + 1, 0:n, :] = r[:, 128:]
        parts = [kvs[(f - t + 4) % 4, 0:n, :] for f in range(4)]
        key = jnp.concatenate([p[:, :64] for p in parts], axis=-1)
        val = jnp.concatenate([p[:, 64:] for p in parts], axis=-1)
        kc[key_rows, :] = rotate(key, cos_t[table, :], sin_t[table, :]).astype(BF16)
        vc[key_rows, :] = val.astype(BF16)

    project_kv(pl.ds(256, PRE), PRE, pl.ds(CL, PRE), pl.ds(CL, PRE), None)

    outs = []
    for cc in range(2):
        rows = pl.ds(128 * cc, 128)
        if cc == 1:
            for copy in st[1]:
                copy.wait_recv()
            norm_cand(1)
        project_kv(rows, CL, pl.ds(0, CL), pl.ds(0, CL), cc)

        def head(r, carry, rows=rows):
            qv = jnp.dot(xn[rows, :], A[r, :, 0:256], preferred_element_type=F32)
            qv = rotate(qv, cos_t[0:CL, :], sin_t[0:CL, :]) * (HS ** -0.5)
            q4[pl.ds(pl.multiple_of(r * CL, CL), CL), :] = qv.astype(BF16)
            return carry

        lax.fori_loop(0, 4, head, 0)
        live = lens[2 * t + cc]

        scores = lax.dot_general(
            q4[...], kc[...], (((1,), (1,)), ((), ())), preferred_element_type=F32
        )
        row = lax.broadcasted_iota(jnp.int32, scores.shape, 0) % CL
        col = lax.broadcasted_iota(jnp.int32, scores.shape, 1)
        scores = jnp.where((col <= row) | (col >= CL), scores, -jnp.inf)
        weights = jnp.exp(scores - jnp.max(scores, axis=-1, keepdims=True))
        divisor = jnp.sum(weights, axis=-1, keepdims=True)
        mix = jnp.dot(weights.astype(BF16), vc[...], preferred_element_type=F32) / divisor
        slot = lax.broadcasted_iota(jnp.int32, mix.shape, 0) % CL
        hr[...] = jnp.where(slot < live, mix, 0.0).astype(BF16)

        def out_cols(n, carry, rows=rows):
            cols = pl.ds(pl.multiple_of(n * 512, 512), 512)
            acc = jnp.zeros((CL, 512), F32)
            for r in range(4):
                acc += jnp.dot(
                    hr[r * CL : (r + 1) * CL, :], B[r, :, cols], preferred_element_type=F32
                )
            ob[rows, cols] = acc.astype(BF16)
            return carry

        lax.fori_loop(0, 4, out_cols, 0)
        outs.append(local(6 + cc, ob.at[rows, :], out.at[rows, :]))

    net.finish()
    for copy in outs:
        copy.wait()


def body(cand_states, prefix_states, norm_gain, w_query, w_key, w_value, w_out, cand_lengths):
    cos_np, sin_np = rope_tables()
    prefix = prefix_states.reshape(8, 128)
    wkv = jnp.concatenate([w_key, w_value], axis=1)
    any_spec = pl.BlockSpec(memory_space=pl.ANY)
    vmem = pl.BlockSpec(memory_space=pltpu.VMEM)
    smem = pl.BlockSpec(memory_space=pltpu.SMEM)
    return pl.pallas_call(
        kernel,
        out_shape=jax.ShapeDtypeStruct((256, D), BF16),
        in_specs=[any_spec, any_spec, vmem, any_spec, any_spec, any_spec, smem, vmem, vmem],
        out_specs=any_spec,
        scratch_shapes=[
            pltpu.VMEM((4, D, 384), BF16),
            pltpu.VMEM((4, HS, D), BF16),
            pltpu.VMEM((1024, FC), BF16),
            pltpu.VMEM((4, 256, FC), BF16),
            pltpu.VMEM((2, 4, 16, 8, 128), BF16),
            pltpu.VMEM((4, 256, 128), F32),
            pltpu.VMEM((320, D), BF16),
            pltpu.VMEM((4, CL, 128), F32),
            pltpu.VMEM((CL + PRE, HS), BF16),
            pltpu.VMEM((CL + PRE, HS), BF16),
            pltpu.VMEM((4 * CL, HS), BF16),
            pltpu.VMEM((4 * CL, HS), BF16),
            pltpu.VMEM((256, D), BF16),
            pltpu.SemaphoreType.DMA((N_SEMS,)),
            pltpu.SemaphoreType.DMA((N_SEMS,)),
            pltpu.SemaphoreType.DMA((8,)),
        ],
        compiler_params=pltpu.CompilerParams(
            collective_id=0, has_side_effects=True, vmem_limit_bytes=56 * 1024 * 1024
        ),
        name="sublayer",
    )(
        cand_states, prefix, norm_gain.reshape(1, D), w_query, wkv, w_out, cand_lengths,
        jnp.asarray(cos_np), jnp.asarray(sin_np),
    )


def solution(mesh):
    in_specs = (
        P(("query", "cand"), "tensor"),
        P(("query", "cand"), "tensor"),
        P(),
        P(None, "tensor"),
        P(None, "tensor"),
        P(None, "tensor"),
        P("tensor", None),
        P(("query", "cand")),
    )
    out_specs = P(("query", "cand", "tensor"), None)
    return jax.shard_map(body, mesh=mesh, in_specs=in_specs, out_specs=out_specs, check_vma=False)
```

time: 257 us -> 74.7 us (0.29)
  waiting for transfers between devices: 131 us -> 0 us
  Pallas kernels: 0 us -> 68.2 us
  blocking collectives: 65.6 us -> 0 us
  matrix products: 15 us -> 0 us
  other arithmetic: 15.3 us -> 1.09 us
  between operations: 13.7 us -> 0.03 us
  starting transfers between devices: 8.3 us -> 0 us
    all_gather x2 -> x0, waiting for transfers between devices: 95.2 us -> none  [the longest x1 95.2 us: in_one_piece(): filled, at, outs = (lax.all_gather(both, axis, axis=dim, tiled=True), 0, [])]
    pallas_call x0 -> x1, Pallas kernels: none -> 68.2 us  [body(): pl.pallas_call(kernel, out_shape=jax.ShapeDtypeStruct((256, D), BF16), in...]
    all_gather x1 -> x0, blocking collectives: 65.6 us -> none  [in_one_piece(): filled, at, outs = (lax.all_gather(both, axis, axis=dim, tiled=True), 0, [])]
    all_to_all x2 -> x0, waiting for transfers between devices: 35.5 us -> none  [the longest x1 21.3 us: from_everyone(): return lax.all_to_all(copies, axis, split_axis=0, concat_axis=0, tiled=True)]
    dot_general x13 -> x0, matrix products: 15 us -> none  [the longest x4 4.42 us: body(): jnp.dot(all_heads[:, head_index * head_size:(head_index + 1) * head_size]...]
    all_to_all x2 -> x0, starting transfers between devices: 8.26 us -> none  [the longest x1 4.73 us: body(): lax.all_to_all(head_rows, 'tensor', split_axis=0, concat_axis=1, tiled=True)]
    convert_element_type x6 -> x0, other arithmetic: 4.78 us -> none  [the longest x1 2.92 us: normalize(): (values * lax.rsqrt(square + epsilon) * norm_gain[None, :]).astype(jnp.bf...]
    reduce_sum x4 -> x0, other arithmetic: 4.11 us -> none  [the longest x2 3.96 us: normalize(): square = jnp.mean(values * values, axis=-1, keepdims=True)]
  transfers between devices with their start and end apart: 4 -> 0, of which waited for: 3 -> 0; matrix products, arithmetic and copies ran while one was open for 6% -> 0% of each run, Pallas kernels for 0% -> 0%
where the time goes in v1:
time: 74.7 us; the launch traced here: 74.4 us
  Pallas kernels  68.2 us (91%)
  local copies, waits for them, and re-layouts  5.13 us (7%)
  other arithmetic  1.09 us (1%)
    pallas_call x1, Pallas kernels, body(): pl.pallas_call(kernel, out_shape=jax.ShapeDtypeStruct((256, D), BF16), in...  68.2 us
    unnamed x5, local copies, waits for them, and re-layouts  3.85 us

profile of v1, /device:TPU:1, one launch (start us, length us, event | category | flops | bytes accessed | tf_op | source)
XLA Modules:
  0.0 74.4 jit_solution(4821822560148816678)
XLA Ops:
  0.0 1.3 %reshape.6.prefix = bf16[8,128]{1,0:T(8,128)(2,1)} reshape(bf16[2,512]{1,0:T(2,128)(2,1)} %param.11) | data formatting | bytes 4096 | tf_op jit(solution)/shard_map/reshape | solution.py:362
  1.3 0.0 copy-start
  1.3 1.3 %copy.11 = bf16[2048,64]{1,0:T(8,128)(2,1)S(1)} copy(bf16[2048,64]{0,1:T(8,128)(2,1)} %param.14) | data formatting | bytes 524288 | tf_op args[4]
  2.6 0.0 copy-done
  2.6 0.3 copy.12
  2.8 1.1 %pad_maximum_fusion.wkv = bf16[2048,128]{1,0:T(8,128)(2,1)} fusion(bf16[2048,64]{1,0:T(8,128)(2,1)S(1)} %copy.12, bf16[2048,64]{1,0:T(8,128)(2,1)S(1)} %copy.11), kind=kLoop, calls=%fused_computation | loop fusion | flops 1048576 | bytes 1048576 | tf_op jit(solution)/shard_map/concatenate | solution.py:363
  3.9 68.2 %sublayer.1 = bf16[256,2048]{1,0:T(8,128)(2,1)} custom-call(bf16[1024,512]{1,0:T(8,128)(2,1)} %states.1, bf16[8,128]{1,0:T(8,128)(2,1)} %reshape.6.prefix, f32[1,2048]{1,0:T(1,128)} %bitcast.1, bf16[2048,256]{1,0:T(8,128)(2,1)} %wq.1, bf16[2048,128]{1,0:T(8,128)(2,1)} %pad_maximum_fusion.wkv, bf16[256,2048]{1,0:T(8,128)(2,1)} %wo.1, s32[8]{0:T(128)} %lens.1, ...), custom_call_target="tpu_custom_call" | custom-call | tf_op jit(solution)/shard_map/sublayer/pallas_call | solution.py:367
  72.1 2.3 %copy.14 = bf16[256,2048]{1,0:T(8,128)(2,1)} copy(bf16[256,2048]{1,0:T(8,128)(2,1)} %sublayer.1) | data formatting | bytes 2097152
Async XLA Ops:
  1.3 1.3 %copy-start = (bf16[2048,64]{0,1:T(8,128)(2,1)S(1)}, bf16[2048,64]{0,1:T(8,128)(2,1)}, u32[]{:S(2)}) copy-start(bf16[2048,64]{0,1:T(8,128)(2,1)} %param.15) | copy-start | bytes 786436

commit v2 on v1

v2 whole, which is shorter than its diff:
```python
import numpy as np

import jax
import jax.numpy as jnp
from jax import lax
from jax.experimental import pallas as pl
from jax.experimental.pallas import tpu as pltpu
from jax.sharding import PartitionSpec as P

MESH = pl.DeviceIdType.MESH
BF16 = jnp.bfloat16
F32 = jnp.float32
EPS = 1e-06
THETA = 10000.0

NX = 4
NY = 4
NZ = 16
ZL = 4
CL = 128
HS = 256
D = 2048
FC = 512
PRE = 64


def rope_tables():
    half = HS // 2
    freq = (THETA ** (-np.arange(half, dtype=np.float32) * 2.0 / HS)).astype(np.float32)
    cand = (PRE + np.arange(CL)).astype(np.float32)
    core, y, zh, r = np.meshgrid(
        np.arange(2), np.arange(4), np.arange(4), np.arange(2), indexing="ij"
    )
    pre = ((zh * 8 + y * 2 + core) * 2 + r).reshape(-1).astype(np.float32)
    pos = np.concatenate([pre, cand])
    angles = (pos[:, None] * freq[None, :]).astype(np.float32).astype(np.float64)
    return np.cos(angles).astype(np.float32), np.sin(angles).astype(np.float32)


class Links:
    def __init__(self, ssem, rsem):
        self.ssem, self.rsem, self.made = ssem, rsem, []

    def send(self, src, dst, device):
        i = len(self.made)
        copy = pltpu.make_async_remote_copy(
            src_ref=src,
            dst_ref=dst,
            send_sem=self.ssem.at[i],
            recv_sem=self.rsem.at[i],
            device_id=device,
            device_id_type=MESH,
        )
        copy.start()
        self.made.append(copy)
        return copy

    def finish(self):
        for copy in self.made:
            copy.wait_send()


N_SEMS = 128
NPRE = PRE


def kernel(
    states, prefix, gain_h, wq, wk, wv, wo, lens_h, cos_h, sin_h,
    out,
    A, B, xs, xb, pb, pf, xn, kvs, kc, vc, q4, hr, ob, gain, cos_t, sin_t, lens,
    ssem, rsem, lsem,
):
    x = lax.axis_index("query")
    cd = lax.axis_index("cand")
    t = lax.axis_index("tensor")
    zh = cd // 8
    y = (cd // 2) % 4
    c = cd % 2
    z = zh * 4 + t

    def at(xx, yy, zz, cc):
        return (xx, (zz // 4) * 8 + yy * 2 + cc, zz % 4)

    def m4(v):
        return (v + 8) % 4

    def zdev(dz):
        return at(x, y, (z + dz + 32) % 16, c)

    def tdev(k):
        return (x, cd, (t + k) % 4)

    xp, xm = at(m4(x + 1), y, z, c), at(m4(x - 1), y, z, c)
    yp, ym = at(x, m4(y + 1), z, c), at(x, m4(y - 1), z, c)
    yo = at(x, m4(y + 2), z, c)
    mate = at(x, y, z, 1 - c)

    def rows_a(xx, yy, off=0, n=64):
        return pl.ds(pl.multiple_of(64 * (c * 16 + yy * 4 + xx) + off, 32), n)

    def cols_b(xx, yy):
        return pl.ds(pl.multiple_of(128 * (xx * 4 + yy), 128), 128)

    def rows_b(off=0, n=192):
        return pl.ds(pl.multiple_of(192 * c + off, 96), n)

    def slice_a(xx, yy, off=0, n=64):
        return A.at[1:4, rows_a(xx, yy, off, n), :]

    def slice_b(xx, yy, off=0, n=192):
        return B.at[1:4, rows_b(off, n), cols_b(xx, yy)]

    def local(i, src, dst):
        copy = pltpu.make_async_copy(src, dst, lsem.at[i])
        copy.start()
        return copy

    lp = local(0, prefix, pb.at[c, y, z])
    lq = local(1, wq, A.at[0])
    lo = [
        local(2, wk, B.at[0, 256:320, :]),
        local(3, wv, B.at[0, 320:384, :]),
        local(4, wo, B.at[0, 0:256, :]),
    ]
    ls = local(5, states, xs)
    lx = local(6, states.at[pl.ds(pl.multiple_of(256 * t, 256), 256), :], xb.at[t])
    small = [
        local(7, gain_h, gain),
        local(8, cos_h, cos_t),
        local(9, sin_h, sin_t),
        local(10, lens_h, lens),
    ]

    net = Links(ssem, rsem)

    lq.wait()
    pa = []
    for k in (2, 1, 3):
        src = A.at[0, rows_a(x, y), :]
        pa.append(net.send(src, A.at[4 - k, rows_a(x, y), :], tdev(k)))
    for copy in lo:
        copy.wait()
    pbq = []
    for k in (2, 1, 3):
        src = B.at[0, rows_b(), cols_b(x, y)]
        pbq.append(net.send(src, B.at[4 - k, rows_b(), cols_b(x, y)], tdev(k)))

    lp.wait()
    tile = pb.at[c, y, z]
    pz = [net.send(tile, tile, zdev(d)) for d in (8, 7, -7, 6, -6, 5, -5, 4, -4, 3, -3, 2, -2, 1, -1)]

    ls.wait()
    st = []
    for cc in range(2):
        part = []
        for k in (2, 1, 3):
            peer = (t + k) % 4
            src = xs.at[pl.ds(pl.multiple_of(256 * peer + 128 * cc, 128), 128), :]
            dst = xb.at[t, pl.ds(128 * cc, 128), :]
            part.append(net.send(src, dst, tdev(k)))
        st.append(part)

    for copy in pa:
        copy.wait_recv()
    own_a, own_b = slice_a(x, y), slice_b(x, y)
    a_xp = net.send(own_a, own_a, xp)
    a_xm = net.send(own_a, own_a, xm)
    for copy in pbq:
        copy.wait_recv()
    b_yp = net.send(own_b, own_b, yp)
    b_ym = net.send(own_b, own_b, ym)
    ya = {0: (net.send(own_a, own_a, yp), net.send(own_a, own_a, ym))}
    xbp = {0: (net.send(own_b, own_b, xp), net.send(own_b, own_b, xm))}

    a_xp.wait_recv()
    h = slice_a(m4(x - 1), y, 0, 32)
    a_xp2 = net.send(h, h, xp)
    s = slice_a(m4(x - 1), y)
    ya[-1] = (net.send(s, s, yp), net.send(s, s, ym))
    a_xm.wait_recv()
    h = slice_a(m4(x + 1), y, 32, 32)
    a_xm2 = net.send(h, h, xm)
    s = slice_a(m4(x + 1), y)
    ya[1] = (net.send(s, s, yp), net.send(s, s, ym))
    b_yp.wait_recv()
    h = slice_b(x, m4(y - 1), 0, 96)
    b_yp2 = net.send(h, h, yp)
    s = slice_b(x, m4(y - 1))
    xbp[-1] = (net.send(s, s, xp), net.send(s, s, xm))
    b_ym.wait_recv()
    h = slice_b(x, m4(y + 1), 96, 96)
    b_ym2 = net.send(h, h, ym)
    s = slice_b(x, m4(y + 1))
    xbp[1] = (net.send(s, s, xp), net.send(s, s, xm))

    a_xp2.wait_recv()
    a_xm2.wait_recv()
    s = slice_a(m4(x + 2), y)
    ya[2] = (net.send(s, s, yp), net.send(s, s, ym))
    b_yp2.wait_recv()
    b_ym2.wait_recv()
    s = slice_b(x, m4(y + 2))
    xbp[2] = (net.send(s, s, xp), net.send(s, s, xm))

    def set_a(yy):
        return A.at[1:4, pl.ds(pl.multiple_of(64 * (c * 16 + yy * 4), 256), 256), :]

    def set_b(xx):
        return B.at[1:4, rows_b(), pl.ds(pl.multiple_of(512 * xx, 512), 512)]

    mates = [net.send(set_a(y), set_a(y), mate), net.send(set_b(x), set_b(x), mate)]

    fwd = {}
    for dx in (0, -1, 1, 2):
        ya[dx][0].wait_recv()
        h = slice_a(m4(x + dx), m4(y - 1), 0, 32)
        f0 = net.send(h, h, yp)
        ya[dx][1].wait_recv()
        h = slice_a(m4(x + dx), m4(y + 1), 32, 32)
        f1 = net.send(h, h, ym)
        xbp[dx][0].wait_recv()
        h = slice_b(m4(x - 1), m4(y + dx), 0, 96)
        f2 = net.send(h, h, xp)
        xbp[dx][1].wait_recv()
        h = slice_b(m4(x + 1), m4(y + dx), 96, 96)
        f3 = net.send(h, h, xm)
        fwd[dx] = (f0, f1, f2, f3)
        if dx == -1:
            for copy in pz:
                copy.wait_recv()
            line = pb.at[c, y]
            py = [net.send(line, line, d) for d in (yo, yp, ym)]
    for s in (set_a(m4(y - 1)), set_a(m4(y + 1)), set_b(m4(x - 1)), set_b(m4(x + 1))):
        mates.append(net.send(s, s, mate))
    for copy in py:
        copy.wait_recv()
    pm = net.send(pb.at[c], pb.at[c], mate)

    lx.wait()
    for copy in small:
        copy.wait()

    def norm_cand(cc):
        rows = pl.ds(128 * cc, 128)
        into = pl.ds(NPRE + 128 * cc, 128)
        total = jnp.zeros((128, 1), F32)
        for f in range(4):
            v = xb[f, rows, :].astype(F32)
            total += jnp.sum(v * v, axis=-1, keepdims=True)
        scale = lax.rsqrt(total * (1.0 / D) + EPS)
        for f in range(4):
            v = xb[f, rows, :].astype(F32)
            g = gain[:, FC * f : FC * (f + 1)]
            xn[into, FC * f : FC * (f + 1)] = (v * scale * g).astype(BF16)

    for copy in st[0]:
        copy.wait_recv()
    norm_cand(0)

    for dx in (0, -1, 1, 2):
        f0, f1, f2, f3 = fwd[dx]
        f0.wait_recv()
        f1.wait_recv()
        s = slice_a(m4(x + dx), m4(y + 2))
        mates.append(net.send(s, s, mate))
        f2.wait_recv()
        f3.wait_recv()
        s = slice_b(m4(x + 2), m4(y + dx))
        mates.append(net.send(s, s, mate))

    pm.wait_recv()
    for f in range(4):
        for g in range(32):
            pf[f, 2 * g : 2 * g + 2, :] = pb[g // 16, (g // 4) % 4, (g % 4) * 4 + f].astype(F32)
    total = jnp.zeros((PRE, 1), F32)
    for f in range(4):
        total += jnp.sum(pf[f] * pf[f], axis=-1, keepdims=True)
    scale = lax.rsqrt(total * (1.0 / D) + EPS)
    for f in range(4):
        g = gain[:, FC * f : FC * (f + 1)]
        xn[0:PRE, FC * f : FC * (f + 1)] = (pf[f] * scale * g).astype(BF16)

    for copy in mates:
        copy.wait_recv()

    def rotate(v, cos, sin):
        a, b = v[:, :128], v[:, 128:]
        return jnp.concatenate([a * cos - b * sin, b * cos + a * sin], axis=-1)

    def project_kv(start, n, first):
        xv = xn[start : start + n, :]
        for pair in range(2):
            w = jnp.concatenate([B[2 * pair, 256:384, :], B[2 * pair + 1, 256:384, :]], axis=0)
            r = lax.dot_general(xv, w, (((1,), (1,)), ((), ())), preferred_element_type=F32)
            kvs[2 * pair, 0:n, :] = r[:, :128]
            kvs[2 * pair + 1, 0:n, :] = r[:, 128:]
        parts = [kvs[(f - t + 4) % 4, 0:n, :] for f in range(4)]
        key = jnp.concatenate([p[:, :64] for p in parts], axis=-1)
        val = jnp.concatenate([p[:, 64:] for p in parts], axis=-1)
        into = pl.ds(first, n)
        kc[into, :] = rotate(key, cos_t[into, :], sin_t[into, :]).astype(BF16)
        vc[into, :] = val.astype(BF16)

    outs = []
    for cc in range(2):
        rows = pl.ds(128 * cc, 128)
        xrows = pl.ds(NPRE + 128 * cc, 128)
        if cc == 0:
            project_kv(0, PRE + CL, 0)
        else:
            for copy in st[1]:
                copy.wait_recv()
            norm_cand(1)
            project_kv(PRE + CL, CL, PRE)

        def head(r, carry, xrows=xrows):
            qv = jnp.dot(xn[xrows, :], A[r], preferred_element_type=F32)
            qv = rotate(qv, cos_t[PRE:, :], sin_t[PRE:, :]) * (HS ** -0.5)
            q4[pl.ds(pl.multiple_of(r * CL, CL), CL), :] = qv.astype(BF16)
            return carry

        lax.fori_loop(0, 4, head, 0)
        live = lens[2 * t + cc]

        scores = lax.dot_general(
            q4[...], kc[...], (((1,), (1,)), ((), ())), preferred_element_type=F32
        )
        row = lax.broadcasted_iota(jnp.int32, scores.shape, 0) % CL
        col = lax.broadcasted_iota(jnp.int32, scores.shape, 1)
        scores = jnp.where(col <= row + PRE, scores, -jnp.inf)
        weights = jnp.exp(scores - jnp.max(scores, axis=-1, keepdims=True))
        divisor = jnp.sum(weights, axis=-1, keepdims=True)
        mix = jnp.dot(weights.astype(BF16), vc[...], preferred_element_type=F32) / divisor
        slot = lax.broadcasted_iota(jnp.int32, mix.shape, 0) % CL
        hr[...] = jnp.where(slot < live, mix, 0.0).astype(BF16)

        def out_cols(n, carry, rows=rows):
            cols = pl.ds(pl.multiple_of(n * 512, 512), 512)
            acc = jnp.zeros((CL, 512), F32)
            for r in range(4):
                acc += jnp.dot(
                    hr[r * CL : (r + 1) * CL, :], B[r, 0:256, cols], preferred_element_type=F32
                )
            ob[rows, cols] = acc.astype(BF16)
            return carry

        lax.fori_loop(0, 4, out_cols, 0)
        outs.append(local(11 + cc, ob.at[rows, :], out.at[rows, :]))

    net.finish()
    for copy in outs:
        copy.wait()


def body(cand_states, prefix_states, norm_gain, w_query, w_key, w_value, w_out, cand_lengths):
    cos_np, sin_np = rope_tables()
    any_spec = pl.BlockSpec(memory_space=pl.ANY)
    return pl.pallas_call(
        kernel,
        out_shape=jax.ShapeDtypeStruct((256, D), BF16),
        in_specs=[any_spec] * 10,
        out_specs=any_spec,
        scratch_shapes=[
            pltpu.VMEM((4, D, HS), BF16),
            pltpu.VMEM((4, 384, D), BF16),
            pltpu.VMEM((1024, FC), BF16),
            pltpu.VMEM((4, 256, FC), BF16),
            pltpu.VMEM((2, 4, 16, 2, FC), BF16),
            pltpu.VMEM((4, PRE, FC), F32),
            pltpu.VMEM((320, D), BF16),
            pltpu.VMEM((4, PRE + CL, 128), F32),
            pltpu.VMEM((CL + PRE, HS), BF16),
            pltpu.VMEM((CL + PRE, HS), BF16),
            pltpu.VMEM((4 * CL, HS), BF16),
            pltpu.VMEM((4 * CL, HS), BF16),
            pltpu.VMEM((256, D), BF16),
            pltpu.VMEM((1, D), F32),
            pltpu.VMEM((PRE + CL, 128), F32),
            pltpu.VMEM((PRE + CL, 128), F32),
            pltpu.SMEM((8,), jnp.int32),
            pltpu.SemaphoreType.DMA((N_SEMS,)),
            pltpu.SemaphoreType.DMA((N_SEMS,)),
            pltpu.SemaphoreType.DMA((16,)),
        ],
        compiler_params=pltpu.CompilerParams(
            has_side_effects=True, vmem_limit_bytes=56 * 1024 * 1024
        ),
        name="sublayer",
    )(
        cand_states, prefix_states, norm_gain.reshape(1, D), w_query, w_key.T, w_value.T,
        w_out, cand_lengths, jnp.asarray(cos_np), jnp.asarray(sin_np),
    )


def solution(mesh):
    in_specs = (
        P(("query", "cand"), "tensor"),
        P(("query", "cand"), "tensor"),
        P(),
        P(None, "tensor"),
        P(None, "tensor"),
        P(None, "tensor"),
        P("tensor", None),
        P(("query", "cand")),
    )
    out_specs = P(("query", "cand", "tensor"), None)
    return jax.shard_map(body, mesh=mesh, in_specs=in_specs, out_specs=out_specs, check_vma=False)
```

time: 74.7 us -> 77.8 us (1.041)
  the two profiles are of different devices: /device:TPU:1 before, /device:TPU:289 now
where the time goes in v2:
time: 77.8 us; the launch traced here: 77.6 us
  Pallas kernels  75.3 us (97%)
  local copies, waits for them, and re-layouts  2.3 us (3%)
    pallas_call x1, Pallas kernels, body(): pl.pallas_call(kernel, out_shape=jax.ShapeDtypeStruct((256, D), BF16), in...  75.3 us
    unnamed x1, local copies, waits for them, and re-layouts  2.3 us

profile of v2, /device:TPU:289, one launch (start us, length us, event | category | flops | bytes accessed | tf_op | source)
XLA Modules:
  0.0 77.6 jit_solution(17194701140633512814)
XLA Ops:
  0.0 75.3 %sublayer.1 = bf16[256,2048]{1,0:T(8,128)(2,1)} custom-call(bf16[1024,512]{1,0:T(8,128)(2,1)} %states.1, bf16[2,512]{1,0:T(2,128)(2,1)} %prefix.1, f32[1,2048]{1,0:T(1,128)} %bitcast.5, bf16[2048,256]{1,0:T(8,128)(2,1)} %wq.1, bf16[64,2048]{1,0:T(8,128)(2,1)} %bitcast.3, bf16[64,2048]{1,0:T(8,128)(2,1)} %bitcast.4, bf16[256,2048]{1,0:T(8,128)(2,1)} %wo.1, ...), custom_call_target="tpu_custom_call" | custom-call | tf_op jit(solution)/shard_map/sublayer/pallas_call | solution.py:358
  75.3 2.3 %copy.12 = bf16[256,2048]{1,0:T(8,128)(2,1)} copy(bf16[256,2048]{1,0:T(8,128)(2,1)} %sublayer.1) | data formatting | bytes 2097152

commit v3 on v2

--- a/solution.py
+++ b/solution.py
@@ -68,7 +68,7 @@
     states, prefix, gain_h, wq, wk, wv, wo, lens_h, cos_h, sin_h,
     out,
     A, B, xs, xb, pb, pf, xn, kvs, kc, vc, q4, hr, ob, gain, cos_t, sin_t, lens,
-    ssem, rsem, lsem,
+    ssem, rsem, lsem, psem, qsem, go,
 ):
     x = lax.axis_index("query")
     cd = lax.axis_index("cand")
@@ -131,7 +131,84 @@
         local(10, lens_h, lens),
     ]
 
+    up_edge = (t == 3) & (zh < 3)
+    down_edge = (t == 0) & (zh > 0)
+    up1, down1 = zdev(1), zdev(-1)
+    barrier = pltpu.get_barrier_semaphore()
+    near = [tdev(1), tdev(2), tdev(3), xp, xm, yp, ym, yo, mate]
+    for device in near:
+        pl.semaphore_signal(barrier, inc=1, device_id=device, device_id_type=MESH)
+
+    @pl.when(up_edge)
+    def _():
+        pl.semaphore_signal(barrier, inc=1, device_id=up1, device_id_type=MESH)
+
+    @pl.when(down_edge)
+    def _():
+        pl.semaphore_signal(barrier, inc=1, device_id=down1, device_id_type=MESH)
+
+    edge = up_edge.astype(jnp.int32) + down_edge.astype(jnp.int32)
+    pl.semaphore_wait(barrier, len(near) + edge)
+
+    @pl.when(up_edge)
+    def _():
+        pl.semaphore_signal(go, inc=1, device_id=up1, device_id_type=MESH)
+
+    @pl.when(down_edge)
+    def _():
+        pl.semaphore_signal(go, inc=1, device_id=down1, device_id_type=MESH)
+
     net = Links(ssem, rsem)
+
+    lp.wait()
+    tile = pb.at[c, y, z]
+    pz = [net.send(tile, tile, tdev(k)) for k in (2, 1, 3)]
+
+    def block_set(b):
+        b = (b + 4) % 4
+        return pb.at[c, y, pl.ds(pl.multiple_of(4 * b, 4), 4)]
+
+    def relay(up, j, k):
+        moved = block_set(zh - j if up else zh + j)
+        return pltpu.make_async_remote_copy(
+            src_ref=moved,
+            dst_ref=moved,
+            send_sem=psem.at[(0 if up else 12) + 4 * j + k - 1],
+            recv_sem=qsem.at[(0 if up else 3) + j],
+            device_id=zdev(k if up else -k),
+            device_id_type=MESH,
+        )
+
+    def relay_start(up, j):
+        here = (up_edge & (zh >= j)) if up else (down_edge & (zh + j <= 3))
+
+        @pl.when(here)
+        def _():
+            if j == 0:
+                pl.semaphore_wait(go, 1)
+            for k in (4, 3, 2, 1):
+                relay(up, j, k).start()
+
+    def relay_sent(up, j):
+        here = (up_edge & (zh >= j)) if up else (down_edge & (zh + j <= 3))
+
+        @pl.when(here)
+        def _():
+            for k in (4, 3, 2, 1):
+                relay(up, j, k).wait_send()
+
+    def relay_arrived(up, j):
+        here = (zh >= j + 1) if up else (zh + j + 1 <= 3)
+
+        @pl.when(here)
+        def _():
+            relay(up, j, 1).wait_recv()
+
+    def relay_step(j):
+        for up in (True, False):
+            relay_arrived(up, j)
+            if j < 2:
+                relay_start(up, j + 1)
 
     lq.wait()
     pa = []
@@ -145,10 +222,6 @@
         src = B.at[0, rows_b(), cols_b(x, y)]
         pbq.append(net.send(src, B.at[4 - k, rows_b(), cols_b(x, y)], tdev(k)))
 
-    lp.wait()
-    tile = pb.at[c, y, z]
-    pz = [net.send(tile, tile, zdev(d)) for d in (8, 7, -7, 6, -6, 5, -5, 4, -4, 3, -3, 2, -2, 1, -1)]
-
     ls.wait()
     st = []
     for cc in range(2):
@@ -171,6 +244,11 @@
     b_ym = net.send(own_b, own_b, ym)
     ya = {0: (net.send(own_a, own_a, yp), net.send(own_a, own_a, ym))}
     xbp = {0: (net.send(own_b, own_b, xp), net.send(own_b, own_b, xm))}
+
+    for copy in pz:
+        copy.wait_recv()
+    relay_start(True, 0)
+    relay_start(False, 0)
 
     a_xp.wait_recv()
     h = slice_a(m4(x - 1), y, 0, 32)
@@ -208,6 +286,7 @@
     def set_b(xx):
         return B.at[1:4, rows_b(), pl.ds(pl.multiple_of(512 * xx, 512), 512)]
 
+    relay_step(0)
     mates = [net.send(set_a(y), set_a(y), mate), net.send(set_b(x), set_b(x), mate)]
 
     fwd = {}
@@ -226,10 +305,10 @@
         f3 = net.send(h, h, xm)
         fwd[dx] = (f0, f1, f2, f3)
         if dx == -1:
-            for copy in pz:
-                copy.wait_recv()
-            line = pb.at[c, y]
-            py = [net.send(line, line, d) for d in (yo, yp, ym)]
+            relay_step(1)
+    relay_step(2)
+    line = pb.at[c, y]
+    py = [net.send(line, line, d) for d in (yo, yp, ym)]
     for s in (set_a(m4(y - 1)), set_a(m4(y + 1)), set_b(m4(x - 1)), set_b(m4(x + 1))):
         mates.append(net.send(s, s, mate))
     for copy in py:
@@ -348,6 +427,9 @@
         outs.append(local(11 + cc, ob.at[rows, :], out.at[rows, :]))
 
     net.finish()
+    for up in (True, False):
+        for j in range(3):
+            relay_sent(up, j)
     for copy in outs:
         copy.wait()
 
@@ -381,9 +463,12 @@
             pltpu.SemaphoreType.DMA((N_SEMS,)),
             pltpu.SemaphoreType.DMA((N_SEMS,)),
             pltpu.SemaphoreType.DMA((16,)),
+            pltpu.SemaphoreType.DMA((24,)),
+            pltpu.SemaphoreType.DMA((6,)),
+            pltpu.SemaphoreType.REGULAR,
         ],
         compiler_params=pltpu.CompilerParams(
-            has_side_effects=True, vmem_limit_bytes=56 * 1024 * 1024
+            collective_id=0, has_side_effects=True, vmem_limit_bytes=56 * 1024 * 1024
         ),
         name="sublayer",
     )(

time: 77.8 us -> 69.6 us (0.89)
  the two profiles are of different devices: /device:TPU:289 before, /device:TPU:1 now
where the time goes in v3:
time: 69.6 us; the launch traced here: 69.4 us
  Pallas kernels  67.1 us (96%)
  local copies, waits for them, and re-layouts  2.3 us (3%)
    pallas_call x1, Pallas kernels, body(): pl.pallas_call(kernel, out_shape=jax.ShapeDtypeStruct((256, D), BF16), in...  67.1 us
    unnamed x1, local copies, waits for them, and re-layouts  2.3 us

profile of v3, /device:TPU:1, one launch (start us, length us, event | category | flops | bytes accessed | tf_op | source)
XLA Modules:
  0.0 69.4 jit_solution(12625907974606846964)
XLA Ops:
  0.0 67.1 %sublayer.1 = bf16[256,2048]{1,0:T(8,128)(2,1)} custom-call(bf16[1024,512]{1,0:T(8,128)(2,1)} %states.1, bf16[2,512]{1,0:T(2,128)(2,1)} %prefix.1, f32[1,2048]{1,0:T(1,128)} %bitcast.5, bf16[2048,256]{1,0:T(8,128)(2,1)} %wq.1, bf16[64,2048]{1,0:T(8,128)(2,1)} %bitcast.3, bf16[64,2048]{1,0:T(8,128)(2,1)} %bitcast.4, bf16[256,2048]{1,0:T(8,128)(2,1)} %wo.1, ...), custom_call_target="tpu_custom_call" | custom-call | tf_op jit(solution)/shard_map/sublayer/pallas_call | solution.py:440
  67.1 2.3 %copy.12 = bf16[256,2048]{1,0:T(8,128)(2,1)} copy(bf16[256,2048]{1,0:T(8,128)(2,1)} %sublayer.1) | data formatting | bytes 2097152

commit v4 on v3

--- a/solution.py
+++ b/solution.py
@@ -60,7 +60,7 @@
             copy.wait_send()
 
 
-N_SEMS = 128
+N_SEMS = 136
 NPRE = PRE
 
 
@@ -68,7 +68,7 @@
     states, prefix, gain_h, wq, wk, wv, wo, lens_h, cos_h, sin_h,
     out,
     A, B, xs, xb, pb, pf, xn, kvs, kc, vc, q4, hr, ob, gain, cos_t, sin_t, lens,
-    ssem, rsem, lsem, psem, qsem, go,
+    ssem, rsem, lsem, psem, qsem, go, chain, go_dn, chain_dn,
 ):
     x = lax.axis_index("query")
     cd = lax.axis_index("cand")
@@ -95,20 +95,26 @@
     yo = at(x, m4(y + 2), z, c)
     mate = at(x, y, z, 1 - c)
 
-    def rows_a(xx, yy, off=0, n=64):
-        return pl.ds(pl.multiple_of(64 * (c * 16 + yy * 4 + xx) + off, 32), n)
-
-    def cols_b(xx, yy):
-        return pl.ds(pl.multiple_of(128 * (xx * 4 + yy), 128), 128)
-
-    def rows_b(off=0, n=192):
-        return pl.ds(pl.multiple_of(192 * c + off, 96), n)
-
-    def slice_a(xx, yy, off=0, n=64):
-        return A.at[1:4, rows_a(xx, yy, off, n), :]
-
-    def slice_b(xx, yy, off=0, n=192):
-        return B.at[1:4, rows_b(off, n), cols_b(xx, yy)]
+    def part_a(s, first, second, off=0, n=32, q=slice(1, 4)):
+        row = c * 1024 + s * 512 + 32 * (second * 4 + first) + off
+        return A.at[q, pl.ds(pl.multiple_of(row, 16), n), :]
+
+    def part_b(s, first, second, off=0, n=96, q=slice(1, 4)):
+        row = 192 * c + 96 * s + off
+        col = 128 * (second * 4 + first)
+        return B.at[
+            q, pl.ds(pl.multiple_of(row, 16), n), pl.ds(pl.multiple_of(col, 128), 128)
+        ]
+
+    def set_a(s, second):
+        row = c * 1024 + s * 512 + 128 * second
+        return A.at[1:4, pl.ds(pl.multiple_of(row, 128), 128), :]
+
+    def set_b(s, second):
+        row, col = 192 * c + 96 * s, 512 * second
+        return B.at[
+            1:4, pl.ds(pl.multiple_of(row, 32), 96), pl.ds(pl.multiple_of(col, 512), 512)
+        ]
 
     def local(i, src, dst):
         copy = pltpu.make_async_copy(src, dst, lsem.at[i])
@@ -150,13 +156,26 @@
     edge = up_edge.astype(jnp.int32) + down_edge.astype(jnp.int32)
     pl.semaphore_wait(barrier, len(near) + edge)
 
+    @pl.when(down_edge)
+    def _():
+        @pl.when(zh == 3)
+        def _():
+            pl.semaphore_signal(go_dn, inc=1, device_id=down1, device_id_type=MESH)
+
+        pl.semaphore_wait(go, 1)
+        pl.semaphore_signal(chain, inc=1, device_id=tdev(3), device_id_type=MESH)
+
     @pl.when(up_edge)
     def _():
+        @pl.when(zh > 0)
+        def _():
+            pl.semaphore_wait(chain, 1)
+
         pl.semaphore_signal(go, inc=1, device_id=up1, device_id_type=MESH)
 
-    @pl.when(down_edge)
-    def _():
-        pl.semaphore_signal(go, inc=1, device_id=down1, device_id_type=MESH)
+    @pl.when((t == 3) & (zh == 3))
+    def _():
+        pl.semaphore_wait(chain, 1)
 
     net = Links(ssem, rsem)
 
@@ -168,59 +187,55 @@
         b = (b + 4) % 4
         return pb.at[c, y, pl.ds(pl.multiple_of(4 * b, 4), 4)]
 
-    def relay(up, j, k):
-        moved = block_set(zh - j if up else zh + j)
+    def spread(k):
+        moved = block_set(zh)
+        far = 1 if abs(k) > 4 else (2 if k > 0 else 0)
         return pltpu.make_async_remote_copy(
             src_ref=moved,
             dst_ref=moved,
-            send_sem=psem.at[(0 if up else 12) + 4 * j + k - 1],
-            recv_sem=qsem.at[(0 if up else 3) + j],
-            device_id=zdev(k if up else -k),
+            send_sem=psem.at[k - 1 if k > 0 else 5 - k],
+            recv_sem=qsem.at[far],
+            device_id=zdev(k),
             device_id_type=MESH,
         )
 
-    def relay_start(up, j):
-        here = (up_edge & (zh >= j)) if up else (down_edge & (zh + j <= 3))
-
-        @pl.when(here)
+    ways = ((3, (6, 5, 4, 3, 2, 1)), (0, (-6, -5, -4, -3, -2, -1)))
+
+    def spread_from(end):
+        for k in ways[0][1] if end == 3 else ways[1][1]:
+            spread(k).start()
+
+    def heard_above(b):
+        @pl.when((t == 3) & (zh == b))
         def _():
-            if j == 0:
-                pl.semaphore_wait(go, 1)
-            for k in (4, 3, 2, 1):
-                relay(up, j, k).start()
-
-    def relay_sent(up, j):
-        here = (up_edge & (zh >= j)) if up else (down_edge & (zh + j <= 3))
-
-        @pl.when(here)
+            pl.semaphore_wait(go_dn, 1)
+            pl.semaphore_signal(chain_dn, inc=1, device_id=tdev(1), device_id_type=MESH)
+            spread_from(3)
+
+    def pass_down(b):
+        @pl.when((t == 0) & (zh == b))
         def _():
-            for k in (4, 3, 2, 1):
-                relay(up, j, k).wait_send()
-
-    def relay_arrived(up, j):
-        here = (zh >= j + 1) if up else (zh + j + 1 <= 3)
-
-        @pl.when(here)
-        def _():
-            relay(up, j, 1).wait_recv()
-
-    def relay_step(j):
-        for up in (True, False):
-            relay_arrived(up, j)
-            if j < 2:
-                relay_start(up, j + 1)
+            pl.semaphore_wait(chain_dn, 1)
+            if b > 0:
+                pl.semaphore_signal(go_dn, inc=1, device_id=down1, device_id_type=MESH)
+            if b < 2:
+                spread_from(0)
+
+    def slices(part, q=slice(1, 4)):
+        return part(0, x, y, q=q), part(1, y, x, q=q)
+
+    def to_peers(part):
+        sent = []
+        for k in (2, 1, 3):
+            for src, dst in zip(slices(part, 0), slices(part, 4 - k)):
+                sent.append(net.send(src, dst, tdev(k)))
+        return sent
 
     lq.wait()
-    pa = []
-    for k in (2, 1, 3):
-        src = A.at[0, rows_a(x, y), :]
-        pa.append(net.send(src, A.at[4 - k, rows_a(x, y), :], tdev(k)))
+    pa = to_peers(part_a)
     for copy in lo:
         copy.wait()
-    pbq = []
-    for k in (2, 1, 3):
-        src = B.at[0, rows_b(), cols_b(x, y)]
-        pbq.append(net.send(src, B.at[4 - k, rows_b(), cols_b(x, y)], tdev(k)))
+    pbq = to_peers(part_b)
 
     ls.wait()
     st = []
@@ -233,87 +248,106 @@
             part.append(net.send(src, dst, tdev(k)))
         st.append(part)
 
+    mates = []
+
+    class Stream:
+        def __init__(self, part, whole, s, n):
+            self.part = lambda i, j, off=0, n=n: part(s, m4(self.me[0] + i), m4(self.me[1] + j), off, n)
+            self.whole = lambda j: whole(s, m4(self.me[1] + j))
+            self.me = (x, y) if s == 0 else (y, x)
+            self.first = (xp, xm) if s == 0 else (yp, ym)
+            self.second = (yp, ym) if s == 0 else (xp, xm)
+            self.half = n // 2
+            self.onward = {}
+
+        def both(self, piece, dirs):
+            return tuple(net.send(piece, piece, d) for d in dirs)
+
+        def own(self):
+            piece = self.part(0, 0)
+            self.near_copies = self.both(piece, self.first)
+            self.onward[0] = self.both(piece, self.second)
+
+        def near(self):
+            self.far_copies = []
+            for side, i in ((0, -1), (1, 1)):
+                self.near_copies[side].wait_recv()
+                h = self.part(i, 0, side * self.half, self.half)
+                self.far_copies.append(net.send(h, h, self.first[side]))
+                self.onward[i] = self.both(self.part(i, 0), self.second)
+
+        def far(self):
+            for copy in self.far_copies:
+                copy.wait_recv()
+            self.onward[2] = self.both(self.part(2, 0), self.second)
+            mates.append(net.send(self.whole(0), self.whole(0), mate))
+
+        def turn(self, i):
+            self.last = getattr(self, "last", {})
+            self.last[i] = []
+            for side, j in ((0, -1), (1, 1)):
+                self.onward[i][side].wait_recv()
+                h = self.part(i, j, side * self.half, self.half)
+                self.last[i].append(net.send(h, h, self.second[side]))
+            if i == 2:
+                for j in (-1, 1):
+                    mates.append(net.send(self.whole(j), self.whole(j), mate))
+
+        def end(self, i):
+            for copy in self.last[i]:
+                copy.wait_recv()
+            s = self.part(i, 2)
+            mates.append(net.send(s, s, mate))
+
+    sa = [Stream(part_a, set_a, s, 32) for s in (0, 1)]
+    sb = [Stream(part_b, set_b, s, 96) for s in (0, 1)]
     for copy in pa:
         copy.wait_recv()
-    own_a, own_b = slice_a(x, y), slice_b(x, y)
-    a_xp = net.send(own_a, own_a, xp)
-    a_xm = net.send(own_a, own_a, xm)
+    for w in sa:
+        w.own()
+    for copy in pz:
+        copy.wait_recv()
+    @pl.when((t == 3) & (zh == 3))
+    def _():
+        spread_from(3)
+
+    @pl.when((t == 0) & (zh >= 2))
+    def _():
+        spread_from(0)
+
+    heard_above(2)
+    for w in sa:
+        w.near()
+    pass_down(2)
     for copy in pbq:
         copy.wait_recv()
-    b_yp = net.send(own_b, own_b, yp)
-    b_ym = net.send(own_b, own_b, ym)
-    ya = {0: (net.send(own_a, own_a, yp), net.send(own_a, own_a, ym))}
-    xbp = {0: (net.send(own_b, own_b, xp), net.send(own_b, own_b, xm))}
-
-    for copy in pz:
-        copy.wait_recv()
-    relay_start(True, 0)
-    relay_start(False, 0)
-
-    a_xp.wait_recv()
-    h = slice_a(m4(x - 1), y, 0, 32)
-    a_xp2 = net.send(h, h, xp)
-    s = slice_a(m4(x - 1), y)
-    ya[-1] = (net.send(s, s, yp), net.send(s, s, ym))
-    a_xm.wait_recv()
-    h = slice_a(m4(x + 1), y, 32, 32)
-    a_xm2 = net.send(h, h, xm)
-    s = slice_a(m4(x + 1), y)
-    ya[1] = (net.send(s, s, yp), net.send(s, s, ym))
-    b_yp.wait_recv()
-    h = slice_b(x, m4(y - 1), 0, 96)
-    b_yp2 = net.send(h, h, yp)
-    s = slice_b(x, m4(y - 1))
-    xbp[-1] = (net.send(s, s, xp), net.send(s, s, xm))
-    b_ym.wait_recv()
-    h = slice_b(x, m4(y + 1), 96, 96)
-    b_ym2 = net.send(h, h, ym)
-    s = slice_b(x, m4(y + 1))
-    xbp[1] = (net.send(s, s, xp), net.send(s, s, xm))
-
-    a_xp2.wait_recv()
-    a_xm2.wait_recv()
-    s = slice_a(m4(x + 2), y)
-    ya[2] = (net.send(s, s, yp), net.send(s, s, ym))
-    b_yp2.wait_recv()
-    b_ym2.wait_recv()
-    s = slice_b(x, m4(y + 2))
-    xbp[2] = (net.send(s, s, xp), net.send(s, s, xm))
-
-    def set_a(yy):
-        return A.at[1:4, pl.ds(pl.multiple_of(64 * (c * 16 + yy * 4), 256), 256), :]
-
-    def set_b(xx):
-        return B.at[1:4, rows_b(), pl.ds(pl.multiple_of(512 * xx, 512), 512)]
-
-    relay_step(0)
-    mates = [net.send(set_a(y), set_a(y), mate), net.send(set_b(x), set_b(x), mate)]
-
-    fwd = {}
-    for dx in (0, -1, 1, 2):
-        ya[dx][0].wait_recv()
-        h = slice_a(m4(x + dx), m4(y - 1), 0, 32)
-        f0 = net.send(h, h, yp)
-        ya[dx][1].wait_recv()
-        h = slice_a(m4(x + dx), m4(y + 1), 32, 32)
-        f1 = net.send(h, h, ym)
-        xbp[dx][0].wait_recv()
-        h = slice_b(m4(x - 1), m4(y + dx), 0, 96)
-        f2 = net.send(h, h, xp)
-        xbp[dx][1].wait_recv()
-        h = slice_b(m4(x + 1), m4(y + dx), 96, 96)
-        f3 = net.send(h, h, xm)
-        fwd[dx] = (f0, f1, f2, f3)
-        if dx == -1:
-            relay_step(1)
-    relay_step(2)
+    for w in sb:
+        w.own()
+    for w in sa:
+        w.far()
+    heard_above(1)
+    pass_down(1)
+    for i in (0, -1, 1, 2):
+        for w in sa:
+            w.turn(i)
+        if i == -1:
+            for w in sb:
+                w.near()
+            heard_above(0)
+            pass_down(0)
+    for w in sb:
+        w.far()
+    for i in (0, -1, 1, 2):
+        for w in sb:
+            w.turn(i)
+        for w in sa:
+            w.end(i)
+    a_mates, mates = mates, []
+
+    for k in (-1, 5, 1):
+        spread(k).wait_recv()
     line = pb.at[c, y]
     py = [net.send(line, line, d) for d in (yo, yp, ym)]
-    for s in (set_a(m4(y - 1)), set_a(m4(y + 1)), set_b(m4(x - 1)), set_b(m4(x + 1))):
-        mates.append(net.send(s, s, mate))
-    for copy in py:
-        copy.wait_recv()
-    pm = net.send(pb.at[c], pb.at[c], mate)
 
     lx.wait()
     for copy in small:
@@ -336,16 +370,32 @@
         copy.wait_recv()
     norm_cand(0)
 
-    for dx in (0, -1, 1, 2):
-        f0, f1, f2, f3 = fwd[dx]
-        f0.wait_recv()
-        f1.wait_recv()
-        s = slice_a(m4(x + dx), m4(y + 2))
-        mates.append(net.send(s, s, mate))
-        f2.wait_recv()
-        f3.wait_recv()
-        s = slice_b(m4(x + 2), m4(y + dx))
-        mates.append(net.send(s, s, mate))
+    for copy in a_mates:
+        copy.wait_recv()
+
+    def rotate(v, cos, sin):
+        a, b = v[:, :128], v[:, 128:]
+        return jnp.concatenate([a * cos - b * sin, b * cos + a * sin], axis=-1)
+
+    def project_q(cc):
+        xrows = pl.ds(NPRE + 128 * cc, 128)
+
+        def head(r, carry):
+            qv = jnp.dot(xn[xrows, :], A[r], preferred_element_type=F32)
+            qv = rotate(qv, cos_t[PRE:, :], sin_t[PRE:, :]) * (HS ** -0.5)
+            q4[pl.ds(pl.multiple_of(r * CL, CL), CL), :] = qv.astype(BF16)
+            return carry
+
+        lax.fori_loop(0, 4, head, 0)
+
+    for copy in py:
+        copy.wait_recv()
+    pm = net.send(pb.at[c], pb.at[c], mate)
+    project_q(0)
+
+    for i in (0, -1, 1, 2):
+        for w in sb:
+            w.end(i)
 
     pm.wait_recv()
     for f in range(4):
@@ -361,10 +411,6 @@
 
     for copy in mates:
         copy.wait_recv()
-
-    def rotate(v, cos, sin):
-        a, b = v[:, :128], v[:, 128:]
-        return jnp.concatenate([a * cos - b * sin, b * cos + a * sin], axis=-1)
 
     def project_kv(start, n, first):
         xv = xn[start : start + n, :]
@@ -383,7 +429,6 @@
     outs = []
     for cc in range(2):
         rows = pl.ds(128 * cc, 128)
-        xrows = pl.ds(NPRE + 128 * cc, 128)
         if cc == 0:
             project_kv(0, PRE + CL, 0)
         else:
@@ -391,14 +436,8 @@
                 copy.wait_recv()
             norm_cand(1)
             project_kv(PRE + CL, CL, PRE)
-
-        def head(r, carry, xrows=xrows):
-            qv = jnp.dot(xn[xrows, :], A[r], preferred_element_type=F32)
-            qv = rotate(qv, cos_t[PRE:, :], sin_t[PRE:, :]) * (HS ** -0.5)
-            q4[pl.ds(pl.multiple_of(r * CL, CL), CL), :] = qv.astype(BF16)
-            return carry
-
-        lax.fori_loop(0, 4, head, 0)
+            project_q(1)
+
         live = lens[2 * t + cc]
 
         scores = lax.dot_general(
@@ -427,9 +466,12 @@
         outs.append(local(11 + cc, ob.at[rows, :], out.at[rows, :]))
 
     net.finish()
-    for up in (True, False):
-        for j in range(3):
-            relay_sent(up, j)
+    for end, ks in ways:
+        @pl.when(t == end)
+        def _(ks=ks):
+            for k in ks:
+                spread(k).wait_send()
+
     for copy in outs:
         copy.wait()
 
@@ -463,8 +505,11 @@
             pltpu.SemaphoreType.DMA((N_SEMS,)),
             pltpu.SemaphoreType.DMA((N_SEMS,)),
             pltpu.SemaphoreType.DMA((16,)),
-            pltpu.SemaphoreType.DMA((24,)),
-            pltpu.SemaphoreType.DMA((6,)),
+            pltpu.SemaphoreType.DMA((12,)),
+            pltpu.SemaphoreType.DMA((3,)),
+            pltpu.SemaphoreType.REGULAR,
+            pltpu.SemaphoreType.REGULAR,
+            pltpu.SemaphoreType.REGULAR,
             pltpu.SemaphoreType.REGULAR,
         ],
         compiler_params=pltpu.CompilerParams(

time: 69.6 us -> 59.8 us (0.86)
  Pallas kernels: 67.1 us -> 57.4 us
    pallas_call x1, Pallas kernels: 67.1 us -> 57.4 us  [body(): pl.pallas_call(kernel, out_shape=jax.ShapeDtypeStruct((256, D), BF16), in...]
where the time goes in v4:
time: 59.8 us; the launch traced here: 59.7 us
  Pallas kernels  57.4 us (96%)
  local copies, waits for them, and re-layouts  2.3 us (4%)
    pallas_call x1, Pallas kernels, body(): pl.pallas_call(kernel, out_shape=jax.ShapeDtypeStruct((256, D), BF16), in...  57.4 us
    unnamed x1, local copies, waits for them, and re-layouts  2.3 us

profile of v4, /device:TPU:1, one launch (start us, length us, event | category | flops | bytes accessed | tf_op | source)
XLA Modules:
  0.0 59.7 jit_solution(5270341775262040902)
XLA Ops:
  0.0 57.4 %sublayer.1 = bf16[256,2048]{1,0:T(8,128)(2,1)} custom-call(bf16[1024,512]{1,0:T(8,128)(2,1)} %states.1, bf16[2,512]{1,0:T(2,128)(2,1)} %prefix.1, f32[1,2048]{1,0:T(1,128)} %bitcast.5, bf16[2048,256]{1,0:T(8,128)(2,1)} %wq.1, bf16[64,2048]{1,0:T(8,128)(2,1)} %bitcast.3, bf16[64,2048]{1,0:T(8,128)(2,1)} %bitcast.4, bf16[256,2048]{1,0:T(8,128)(2,1)} %wo.1, ...), custom_call_target="tpu_custom_call" | custom-call | tf_op jit(solution)/shard_map/sublayer/pallas_call | solution.py:482
  57.4 2.3 %copy.12 = bf16[256,2048]{1,0:T(8,128)(2,1)} copy(bf16[256,2048]{1,0:T(8,128)(2,1)} %sublayer.1) | data formatting | bytes 2097152

commit v5 on v4

--- a/solution.py
+++ b/solution.py
@@ -383,7 +383,7 @@
         def head(r, carry):
             qv = jnp.dot(xn[xrows, :], A[r], preferred_element_type=F32)
             qv = rotate(qv, cos_t[PRE:, :], sin_t[PRE:, :]) * (HS ** -0.5)
-            q4[pl.ds(pl.multiple_of(r * CL, CL), CL), :] = qv.astype(BF16)
+            q4[cc, pl.ds(pl.multiple_of(r * CL, CL), CL), :] = qv.astype(BF16)
             return carry
 
         lax.fori_loop(0, 4, head, 0)
@@ -393,7 +393,7 @@
     pm = net.send(pb.at[c], pb.at[c], mate)
     project_q(0)
 
-    for i in (0, -1, 1, 2):
+    for i in (0, -1):
         for w in sb:
             w.end(i)
 
@@ -409,61 +409,63 @@
         g = gain[:, FC * f : FC * (f + 1)]
         xn[0:PRE, FC * f : FC * (f + 1)] = (pf[f] * scale * g).astype(BF16)
 
+    for copy in st[1]:
+        copy.wait_recv()
+    norm_cand(1)
+    project_q(1)
+
+    for i in (1, 2):
+        for w in sb:
+            w.end(i)
     for copy in mates:
         copy.wait_recv()
 
-    def project_kv(start, n, first):
-        xv = xn[start : start + n, :]
-        for pair in range(2):
-            w = jnp.concatenate([B[2 * pair, 256:384, :], B[2 * pair + 1, 256:384, :]], axis=0)
-            r = lax.dot_general(xv, w, (((1,), (1,)), ((), ())), preferred_element_type=F32)
-            kvs[2 * pair, 0:n, :] = r[:, :128]
-            kvs[2 * pair + 1, 0:n, :] = r[:, 128:]
-        parts = [kvs[(f - t + 4) % 4, 0:n, :] for f in range(4)]
-        key = jnp.concatenate([p[:, :64] for p in parts], axis=-1)
-        val = jnp.concatenate([p[:, 64:] for p in parts], axis=-1)
-        into = pl.ds(first, n)
-        kc[into, :] = rotate(key, cos_t[into, :], sin_t[into, :]).astype(BF16)
-        vc[into, :] = val.astype(BF16)
-
-    outs = []
+    for pair in range(2):
+        w = jnp.concatenate([B[2 * pair, 256:384, :], B[2 * pair + 1, 256:384, :]], axis=0)
+        r = lax.dot_general(xn[...], w, (((1,), (1,)), ((), ())), preferred_element_type=F32)
+        kvs[2 * pair] = r[:, :128]
+        kvs[2 * pair + 1] = r[:, 128:]
+    parts = [kvs[(f - t + 4) % 4] for f in range(4)]
+    key = jnp.concatenate([p[:, :64] for p in parts], axis=-1)
+    vc[...] = jnp.concatenate([p[:, 64:] for p in parts], axis=-1).astype(BF16)
+    kc[0 : PRE + CL, :] = rotate(key[: PRE + CL], cos_t[...], sin_t[...]).astype(BF16)
+    kc[PRE + CL :, :] = rotate(key[PRE + CL :], cos_t[PRE:, :], sin_t[PRE:, :]).astype(BF16)
+
     for cc in range(2):
-        rows = pl.ds(128 * cc, 128)
-        if cc == 0:
-            project_kv(0, PRE + CL, 0)
-        else:
-            for copy in st[1]:
-                copy.wait_recv()
-            norm_cand(1)
-            project_kv(PRE + CL, CL, PRE)
-            project_q(1)
-
+        own = PRE + CL * cc
+        keys = jnp.concatenate([kc[0:PRE, :], kc[own : own + CL, :]], axis=0)
+        vals = jnp.concatenate([vc[0:PRE, :], vc[own : own + CL, :]], axis=0)
         live = lens[2 * t + cc]
-
         scores = lax.dot_general(
-            q4[...], kc[...], (((1,), (1,)), ((), ())), preferred_element_type=F32
+            q4[cc], keys, (((1,), (1,)), ((), ())), preferred_element_type=F32
         )
         row = lax.broadcasted_iota(jnp.int32, scores.shape, 0) % CL
         col = lax.broadcasted_iota(jnp.int32, scores.shape, 1)
         scores = jnp.where(col <= row + PRE, scores, -jnp.inf)
         weights = jnp.exp(scores - jnp.max(scores, axis=-1, keepdims=True))
         divisor = jnp.sum(weights, axis=-1, keepdims=True)
-        mix = jnp.dot(weights.astype(BF16), vc[...], preferred_element_type=F32) / divisor
+        mix = jnp.dot(weights.astype(BF16), vals, preferred_element_type=F32) / divisor
         slot = lax.broadcasted_iota(jnp.int32, mix.shape, 0) % CL
-        hr[...] = jnp.where(slot < live, mix, 0.0).astype(BF16)
-
-        def out_cols(n, carry, rows=rows):
-            cols = pl.ds(pl.multiple_of(n * 512, 512), 512)
-            acc = jnp.zeros((CL, 512), F32)
-            for r in range(4):
-                acc += jnp.dot(
-                    hr[r * CL : (r + 1) * CL, :], B[r, 0:256, cols], preferred_element_type=F32
-                )
-            ob[rows, cols] = acc.astype(BF16)
-            return carry
-
-        lax.fori_loop(0, 4, out_cols, 0)
-        outs.append(local(11 + cc, ob.at[rows, :], out.at[rows, :]))
+        mix = jnp.where(slot < live, mix, 0.0).astype(BF16)
+        for r in range(4):
+            hr[CL * cc : CL * (cc + 1), HS * r : HS * (r + 1)] = mix[r * CL : (r + 1) * CL]
+
+    def out_cols(n, carry):
+        cols = pl.ds(pl.multiple_of(n * 512, 512), 512)
+        acc = jnp.zeros((256, 512), F32)
+        for r in range(4):
+            acc += jnp.dot(
+                hr[:, HS * r : HS * (r + 1)], B[r, 0:256, cols], preferred_element_type=F32
+            )
+        ob[:, cols] = acc.astype(BF16)
+        pltpu.make_async_copy(ob.at[:, cols], out.at[:, cols], lsem.at[11 + n]).start()
+        return carry
+
+    lax.fori_loop(0, 4, out_cols, 0)
+    outs = []
+    for n in range(4):
+        cols = pl.ds(n * 512, 512)
+        outs.append(pltpu.make_async_copy(ob.at[:, cols], out.at[:, cols], lsem.at[11 + n]))
 
     net.finish()
     for end, ks in ways:
@@ -492,11 +494,11 @@
             pltpu.VMEM((2, 4, 16, 2, FC), BF16),
             pltpu.VMEM((4, PRE, FC), F32),
             pltpu.VMEM((320, D), BF16),
-            pltpu.VMEM((4, PRE + CL, 128), F32),
-            pltpu.VMEM((CL + PRE, HS), BF16),
-            pltpu.VMEM((CL + PRE, HS), BF16),
-            pltpu.VMEM((4 * CL, HS), BF16),
-            pltpu.VMEM((4 * CL, HS), BF16),
+            pltpu.VMEM((4, 320, 128), F32),
+            pltpu.VMEM((320, HS), BF16),
+            pltpu.VMEM((320, HS), BF16),
+            pltpu.VMEM((2, 4 * CL, HS), BF16),
+            pltpu.VMEM((256, 4 * HS), BF16),
             pltpu.VMEM((256, D), BF16),
             pltpu.VMEM((1, D), F32),
             pltpu.VMEM((PRE + CL, 128), F32),

time: 59.8 us -> 57.9 us (0.968)
  Pallas kernels: 57.4 us -> 55.4 us
    pallas_call x1, Pallas kernels: 57.4 us -> 55.4 us  [body(): pl.pallas_call(kernel, out_shape=jax.ShapeDtypeStruct((256, D), BF16), in...]
where the time goes in v5:
time: 57.9 us; the launch traced here: 57.7 us
  Pallas kernels  55.4 us (96%)
  local copies, waits for them, and re-layouts  2.3 us (4%)
    pallas_call x1, Pallas kernels, body(): pl.pallas_call(kernel, out_shape=jax.ShapeDtypeStruct((256, D), BF16), in...  55.4 us
    unnamed x1, local copies, waits for them, and re-layouts  2.3 us

profile of v5, /device:TPU:1, one launch (start us, length us, event | category | flops | bytes accessed | tf_op | source)
XLA Modules:
  0.0 57.7 jit_solution(18284095234715768722)
XLA Ops:
  0.0 55.4 %sublayer.1 = bf16[256,2048]{1,0:T(8,128)(2,1)} custom-call(bf16[1024,512]{1,0:T(8,128)(2,1)} %states.1, bf16[2,512]{1,0:T(2,128)(2,1)} %prefix.1, f32[1,2048]{1,0:T(1,128)} %bitcast.5, bf16[2048,256]{1,0:T(8,128)(2,1)} %wq.1, bf16[64,2048]{1,0:T(8,128)(2,1)} %bitcast.3, bf16[64,2048]{1,0:T(8,128)(2,1)} %bitcast.4, bf16[256,2048]{1,0:T(8,128)(2,1)} %wo.1, ...), custom_call_target="tpu_custom_call" | custom-call | tf_op jit(solution)/shard_map/sublayer/pallas_call | solution.py:484
  55.4 2.3 %copy.12 = bf16[256,2048]{1,0:T(8,128)(2,1)} copy(bf16[256,2048]{1,0:T(8,128)(2,1)} %sublayer.1) | data formatting | bytes 2097152

commit v6 on v5

--- a/solution.py
+++ b/solution.py
@@ -409,14 +409,15 @@
         g = gain[:, FC * f : FC * (f + 1)]
         xn[0:PRE, FC * f : FC * (f + 1)] = (pf[f] * scale * g).astype(BF16)
 
-    for copy in st[1]:
-        copy.wait_recv()
-    norm_cand(1)
-    project_q(1)
-
     for i in (1, 2):
         for w in sb:
             w.end(i)
+
+    for copy in st[1]:
+        copy.wait_recv()
+    norm_cand(1)
+    project_q(1)
+
     for copy in mates:
         copy.wait_recv()
 

time: 57.9 us -> 56.4 us (0.974)
  Pallas kernels: 55.4 us -> 53.9 us
    pallas_call x1, Pallas kernels: 55.4 us -> 53.9 us  [body(): pl.pallas_call(kernel, out_shape=jax.ShapeDtypeStruct((256, D), BF16), in...]
where the time goes in v6:
time: 56.4 us; the launch traced here: 56.2 us
  Pallas kernels  53.9 us (96%)
  local copies, waits for them, and re-layouts  2.3 us (4%)
    pallas_call x1, Pallas kernels, body(): pl.pallas_call(kernel, out_shape=jax.ShapeDtypeStruct((256, D), BF16), in...  53.9 us
    unnamed x1, local copies, waits for them, and re-layouts  2.3 us

profile of v6, /device:TPU:1, one launch (start us, length us, event | category | flops | bytes accessed | tf_op | source)
XLA Modules:
  0.0 56.2 jit_solution(9187274279011713685)
XLA Ops:
  0.0 53.9 %sublayer.1 = bf16[256,2048]{1,0:T(8,128)(2,1)} custom-call(bf16[1024,512]{1,0:T(8,128)(2,1)} %states.1, bf16[2,512]{1,0:T(2,128)(2,1)} %prefix.1, f32[1,2048]{1,0:T(1,128)} %bitcast.5, bf16[2048,256]{1,0:T(8,128)(2,1)} %wq.1, bf16[64,2048]{1,0:T(8,128)(2,1)} %bitcast.3, bf16[64,2048]{1,0:T(8,128)(2,1)} %bitcast.4, bf16[256,2048]{1,0:T(8,128)(2,1)} %wo.1, ...), custom_call_target="tpu_custom_call" | custom-call | tf_op jit(solution)/shard_map/sublayer/pallas_call | solution.py:485
  53.9 2.3 %copy.12 = bf16[256,2048]{1,0:T(8,128)(2,1)} copy(bf16[256,2048]{1,0:T(8,128)(2,1)} %sublayer.1) | data formatting | bytes 2097152
